TPU v7x, 32 devices: a whole 2x2x4 slice. The times are simulated.
32 devices in a mesh: row: 4 (over x, core), col: 8 (over z, y).
Axes of the slice: x: 2, y: 2, z: 4, core: 2. Of those that a mesh axis runs over, the one named last changes fastest.
Arguments:
- counts: float32 [8192, 8192], P('row', 'col'), may hold values from 0 to 514, as said below
- labels: int32 [983040], replicated, may hold values from 0 to 8191, as said below
- edge_tiles: int32 [1024, 2, 128], P(('row', 'col')), may hold values from 0 to 983039, as said below
- proposals: int32 [2, 128], replicated, may hold values from 0 to 8191, as said below
- accept_flags: int32 [128], P('col'), may hold values 0 or 1
Outputs:
- count_matrix: float32 [8192, 8192], P('row', 'col')
- merge_cost: float32 [128], P('col')
- accepted_cost: float32 [128], P('col')
Inputs may be any that keep to these rules, and one draw needn't show every extreme that they name: `counts`: Symmetric, whole numbers, every diagonal entry at least 2. `labels`: every block holds exactly 120 vertices. `edge_tiles`: each edge gives the two entries (label of its first vertex, label of its second) and the reverse; entry (r, s) lies in tile (r // 2048, s // 1024). Of the 8192 entries of one device's edges at most 576 lie in one tile, and in every draw some tile gets exactly 576 entries from every device. proposals[1, p] differs from proposals[0, p]; for p // 16 = c, proposals[0, p] lies in c * 1024 to (c + 1) * 1024 - 1, and these sources are distinct.
All inputs are finite; a program needn't handle non-finite values. No bound on the sum of `accept_flags` on one device may be relied on, other than what follows from the above.
Results may differ from a plain program's by a relative error of at most 0.0003.
Values sent between devices are 32-bit elements; how exact they have to be, the bound alone decides.
No kernel may reach another device: no remote copies, remote signals or barrier semaphores. Data moves between devices by JAX's collectives and lax.ppermute only.
A program may use at most 128 MiB of HBM per device.

v0:
```python
import jax
import jax.numpy as jnp
from jax import lax
from jax.sharding import PartitionSpec as P

BLOCKS = 8192
PROP_COL = 16


def entropy_term(value):
    return value * jnp.log(jnp.maximum(value, 1.0))


def per_device(counts, labels, edge_tiles, proposals, accept_flags):
    rows_tile = counts.shape[0]
    cols_tile = counts.shape[1]
    row_devices = lax.axis_size("row")
    col_devices = lax.axis_size("col")
    devices = row_devices * col_devices
    edge_count = edge_tiles.shape[0] * edge_tiles.shape[2]
    capacity = 9 * edge_count // (2 * devices)
    first_label = labels[edge_tiles[:, 0, :].reshape(-1)]
    second_label = labels[edge_tiles[:, 1, :].reshape(-1)]
    row_block = jnp.concatenate([first_label, second_label])
    col_block = jnp.concatenate([second_label, first_label])
    entry_count = row_block.shape[0]
    owners = row_block // rows_tile * col_devices + col_block // cols_tile
    owner_match = owners[:, None] == jnp.arange(devices, dtype=jnp.int32)[None, :]
    block_rows = 512
    block_ids = jnp.arange(block_rows, dtype=jnp.int32)
    lower = (block_ids[:, None] >= block_ids[None, :]).astype(jnp.bfloat16)
    stacked_hot = owner_match.astype(jnp.bfloat16).reshape(
        entry_count // block_rows, block_rows, devices
    )
    within = jnp.einsum("ij,bjd->bid", lower, stacked_hot, preferred_element_type=jnp.float32)
    totals = within[:, -1, :]
    earlier = jnp.cumsum(totals, axis=0) - totals
    running = (within + earlier[:, None, :]).reshape(entry_count, devices)
    slot_rank = jnp.sum(jnp.where(owner_match, running, jnp.float32(0.0)), axis=1) - 1.0
    slot_hot = (slot_rank[:, None] == jnp.arange(capacity, dtype=jnp.float32)[None, :]).astype(
        jnp.float32
    )
    row_value = (row_block % rows_tile + 1).astype(jnp.float32)
    col_value = (col_block % cols_tile + 1).astype(jnp.float32)
    carried = jnp.concatenate(
        [slot_hot * row_value[:, None], slot_hot * col_value[:, None]], axis=1
    )
    placed = lax.dot_general(
        owner_match.astype(jnp.float32),
        carried,
        (((0,), (0,)), ((), ())),
        precision=lax.Precision.HIGHEST,
        preferred_element_type=jnp.float32,
    )
    outgoing = placed.reshape(devices, 2, capacity).astype(jnp.int32) - 1
    arrived = lax.all_to_all(outgoing, ("row", "col"), split_axis=0, concat_axis=0, tiled=True)
    per_group = 16
    grouped = arrived.reshape(devices // per_group, per_group, 2, capacity)
    row_ids = jnp.arange(rows_tile, dtype=jnp.int32)
    col_ids = jnp.arange(cols_tile, dtype=jnp.int32)

    def add_group(running_sum, arrived_block):
        wanted_rows = arrived_block[:, 0, :].reshape(-1)
        wanted_cols = arrived_block[:, 1, :].reshape(-1)
        row_hot = (row_ids[:, None] == wanted_rows[None, :]).astype(jnp.bfloat16)
        col_hot = (wanted_cols[:, None] == col_ids[None, :]).astype(jnp.bfloat16)
        return (running_sum + jnp.dot(row_hot, col_hot, preferred_element_type=jnp.float32), None)

    increments, _ = lax.scan(add_group, jnp.zeros((rows_tile, cols_tile), jnp.float32), grouped)
    updated = counts + increments
    col_index = lax.axis_index("col")
    row_index = lax.axis_index("row")
    mine = lax.dynamic_slice_in_dim(proposals, col_index * PROP_COL, PROP_COL, 1)
    source = mine[0]
    target = mine[1]
    own_selector = (source[:, None] == col_index * cols_tile + col_ids[None, :]).astype(jnp.float32)
    own_column = lax.dot_general(
        own_selector,
        updated,
        (((1,), (1,)), ((), ())),
        precision=lax.Precision.HIGHEST,
        preferred_element_type=jnp.float32,
    )
    all_targets = proposals[1]
    selector = (all_targets[:, None] == col_index * cols_tile + col_ids[None, :]).astype(
        jnp.float32
    )
    other_column = lax.psum_scatter(
        lax.dot_general(
            selector,
            updated,
            (((1,), (1,)), ((), ())),
            precision=lax.Precision.HIGHEST,
            preferred_element_type=jnp.float32,
        ),
        "col",
        scatter_dimension=0,
        tiled=True,
    )
    row_global = row_index * rows_tile + row_ids
    at_source = row_global[None, :] == source[:, None]
    at_target = row_global[None, :] == target[:, None]
    mixed = (
        entropy_term(own_column + other_column)
        - entropy_term(own_column)
        - entropy_term(other_column)
    )
    pair_part = jnp.sum(jnp.where(at_source | at_target, jnp.float32(0.0), mixed), axis=1)
    source_part = jnp.sum(jnp.where(at_source, own_column, jnp.float32(0.0)), axis=1)
    cross_part = jnp.sum(jnp.where(at_source, other_column, jnp.float32(0.0)), axis=1)
    target_part = jnp.sum(jnp.where(at_target, other_column, jnp.float32(0.0)), axis=1)
    degree_part = jnp.sum(own_column, axis=1)
    other_degree = jnp.sum(other_column, axis=1)
    pair_sum, self_source, cross_count, self_target, degree_source, degree_target = lax.psum(
        (pair_part, source_part, cross_part, target_part, degree_part, other_degree), "row"
    )
    corner = (
        entropy_term(self_source + 2.0 * cross_count + self_target)
        - entropy_term(self_source)
        - entropy_term(self_target)
        - 2.0 * entropy_term(cross_count)
    )
    change = (
        -(pair_sum + 0.5 * corner)
        + entropy_term(degree_source + degree_target)
        - entropy_term(degree_source)
        - entropy_term(degree_target)
    )
    merge_cost = change / BLOCKS
    accepted_cost = jnp.where(accept_flags == 1, merge_cost, jnp.float32(0.0))
    return (updated, merge_cost, accepted_cost)


def solution(mesh):
    return jax.shard_map(
        per_device,
        mesh=mesh,
        in_specs=(P("row", "col"), P(), P(("row", "col"), None, None), P(), P("col")),
        out_specs=(P("row", "col"), P("col"), P("col")),
        check_vma=False,
    )
```

profile of v0, /device:TPU:0, one launch (start us, length us, event | category | flops | bytes accessed | tf_op | source)
XLA Modules:
  0.0 404.8 jit_solution(17669434263731463338)
XLA Ops:
  7.2 0.9 compare_select_fusion.4
  8.1 52.1 %gather_fusion = s32[4096]{0:T(1024)S(1)} fusion(s32[983040]{0:T(1024)} %param.8, s32[4096]{0:T(1024)S(1)} %broadcast_clamp_fusion.1), kind=kCustom, calls=%fused_computation | custom fusion | bytes 49152 | tf_op jit(solution)/shard_map/gather | solution.py:22
  60.2 52.1 %gather_fusion.1 = s32[4096]{0:T(1024)S(1)} fusion(s32[983040]{0:T(1024)} %param.8, s32[4096]{0:T(1024)S(1)} %broadcast_clamp_fusion), kind=kCustom, calls=%fused_computation.1 | custom fusion | bytes 49152 | tf_op jit(solution)/shard_map/gather | solution.py:23
  112.5 0.5 convolution_bitcast_fusion
  113.5 0.3 subtract_reduce_fusion
  113.8 0.3 select_reduce_fusion
  114.2 12.6 %fusion.12 = (f32[8192,576]{0,1:T(8,128)}, f32[8192,576]{0,1:T(8,128)}) fusion(f32[8192]{0:T(1024)S(1)} %get-tuple-element.73, f32[8192]{0:T(1024)S(1)} %bitcast.36, f32[8192]{0:T(1024)S(1)} %get-tuple-element.72), kind=kLoop, calls=%fused_computation.19 | loop fusion | flops 14155776 | bytes 37847040 | tf_op jit(solution)/shard_map/mul | solution.py:46
  126.9 22.8 %fusion.16 = s32[32,1152]{1,0:T(8,128)S(1)} fusion(f32[8192,576]{0,1:T(8,128)} %get-tuple-element.75, f32[8192,576]{0,1:T(8,128)} %get-tuple-element.74, s32[8192]{0:T(1024)S(1)} %get-tuple-element.71), kind=kOutput, calls=%fused_computation.21 | convolution fusion | flops 3633651712 | bytes 37928960 | tf_op jit(solution)/shard_map/dot_general | solution.py:48
  149.7 0.8 sub.59
  150.5 7.3 %all-to-all-start = ((s32[32,2,576]{2,1,0:T(2,128)}), s32[32,2,576]{2,1,0:T(2,128)S(1)}, u32[]{:S(2)}, u32[]{:S(2)}) async-start(s32[32,2,576]{2,1,0:T(2,128)} %sub.59), calls=%async_computation | async-start | bytes 327680 | tf_op jit(solution)/shard_map/all_to_all | solution.py:56
  158.1 0.6 iota_add_fusion.1
  158.7 0.5 slice_bitcast_fusion
  159.2 6.6 %all-to-all-done = s32[32,2,576]{2,1,0:T(2,128)S(1)} async-done(((s32[32,2,576]{2,1,0:T(2,128)}), s32[32,2,576]{2,1,0:T(2,128)S(1)}, u32[]{:S(2)}, u32[]{:S(2)}) %all-to-all-start) | async-done | bytes 147488 | tf_op jit(solution)/shard_map/all_to_all | solution.py:56
  165.8 134.2 %while.11 = (s32[]{:T(128)}, f32[2048,1024]{1,0:T(8,128)}, s32[2,16,2,576]{3,2,1,0:T(2,128)S(1)}, s32[]{:T(128)}, s32[]{:T(128)}) while((s32[]{:T(128)}, f32[2048,1024]{1,0:T(8,128)}, s32[2,16,2,576]{3,2,1,0:T(2,128)S(1)}, s32[]{:T(128)}, s32[]{:T(128)}) %tuple.47), condition=%wide.region_3.4_spmd.clone, body=%wide.region_2.3_spmd.clone.sunk | while | flops 38687211520 | bytes 36167752 | solution.py:69
  166.1 7.1 %iota_compare_fusion.24 = pred[9216,1024]{1,0:T(32,128)(4,1)} fusion(s32[9216]{0:T(1024)S(1)} %eq.287), kind=kLoop, calls=%fused_computation.6.clone.clone.clone.clone.2.clone.1 | loop fusion | flops 9437184 | bytes 9474048 | tf_op jit(solution)/shard_map/while/body/eval_jaxpr/dot_general | solution.py:67
  173.3 59.5 %select_add_fusion.2 = f32[2048,1024]{1,0:T(8,128)} fusion(f32[2048,1024]{1,0:T(8,128)} %get-tuple-element.111, s32[9216]{0:T(1024)S(1)} %eq.286, pred[]{:T(512)S(6)} %compare.27, pred[9216,1024]{1,0:T(32,128)(4,1)} %iota_compare_fusion.24), kind=kOutput, calls=%fused_computation.9.clone.3 | convolution fusion | flops 38677774336 | bytes 26251264 | tf_op jit(solution)/shard_map/while/body/eval_jaxpr/dot_general | solution.py:67
  233.1 7.1 %iota_compare_fusion.24 = pred[9216,1024]{1,0:T(32,128)(4,1)} fusion(s32[9216]{0:T(1024)S(1)} %eq.287), kind=kLoop, calls=%fused_computation.6.clone.clone.clone.clone.2.clone.1 | loop fusion | flops 9437184 | bytes 9474048 | tf_op jit(solution)/shard_map/while/body/eval_jaxpr/dot_general | solution.py:67
  240.2 59.8 %select_add_fusion.2 = f32[2048,1024]{1,0:T(8,128)} fusion(f32[2048,1024]{1,0:T(8,128)} %get-tuple-element.111, s32[9216]{0:T(1024)S(1)} %eq.286, pred[]{:T(512)S(6)} %compare.27, pred[9216,1024]{1,0:T(32,128)(4,1)} %iota_compare_fusion.24), kind=kOutput, calls=%fused_computation.9.clone.3 | convolution fusion | flops 38677774336 | bytes 26251264 | tf_op jit(solution)/shard_map/while/body/eval_jaxpr/dot_general | solution.py:67
  300.0 12.2 %add.170 = f32[2048,1024]{1,0:T(8,128)} add(f32[2048,1024]{1,0:T(8,128)} %param.7, f32[2048,1024]{1,0:T(8,128)} %get-tuple-element.30) | non-fusion elementwise | flops 2097152 | bytes 25165824 | tf_op jit(solution)/shard_map/add | solution.py:70
  312.2 9.2 %fusion.23 = f32[128,2048]{1,0:T(8,128)} fusion(f32[2048,1024]{1,0:T(8,128)} %add.170, s32[1024]{0:T(1024)S(1)} %copy-done, s32[128]{0:T(128)S(1)} %copy-done.3), kind=kOutput, calls=%fused_computation.30 | convolution fusion | flops 3221356544 | bytes 9441792 | tf_op jit(solution)/shard_map/dot_general | solution.py:89
  321.5 62.9 %reduce-scatter.2.cloned.1.call-done = f32[16,2048]{1,0:T(8,128)} async-done(((f32[128,2048]{1,0:T(8,128)}), f32[16,2048]{1,0:T(8,128)}) %reduce-scatter.2.cloned.1.call-update) | async-done | bytes 131088 | tf_op jit(solution)/shard_map/reduce_scatter | solution.py:88
  384.4 7.4 %fusion.28 = (f32[16]{0:T(128)S(1)}, f32[16]{0:T(128)S(1)}, f32[16]{0:T(128)S(1)}, f32[16]{0:T(128)S(1)}, f32[16]{0:T(128)S(1)}, /*index=5*/f32[16]{0:T(128)S(1)}) fusion(s32[2048]{0:T(1024)S(1)} %iota_add_fusion, s32[16]{0:T(128)S(1)} %get-tuple-element.81, f32[16,2048]{1,0:T(8,128)} %reduce-scatter.2.cloned.1.call-done, s32[16]{0:T(128)S(1)} %get-tuple-element.80, ...), kind=kOutput, calls=%fused_computation.40 | convolution fusion | flops 403390368 | bytes 8532480 | tf_op jit(solution)/shard_map/dot_general | solution.py:77
  391.8 5.7 %all-reduce = (f32[16]{0:T(128)S(1)}, f32[16]{0:T(128)S(1)}, f32[16]{0:T(128)S(1)}, f32[16]{0:T(128)S(1)}, f32[16]{0:T(128)S(1)}, /*index=5*/f32[16]{0:T(128)S(1)}) all-reduce(f32[16]{0:T(128)S(1)} %get-tuple-element.53, f32[16]{0:T(128)S(1)} %get-tuple-element.54, ...), channel_id=1, replica_groups=mesh['row'=4,'col'=8] {'row'}, use_global_device_ids=true, to_apply=%region_16.17 | all-reduce | flops 96 | bytes 768 | tf_op jit(solution)/shard_map/psum | solution.py:114
  397.4 0.5 compare_select_fusion.5
  (40 shorter events, 1.9 us)
Async XLA Ops:
  126.9 31.8 %copy-start.1 = (s32[2,128]{1,0:T(2,128)S(1)}, s32[2,128]{1,0:T(2,128)}, u32[]{:S(2)}) copy-start(s32[2,128]{1,0:T(2,128)} %param.10) | copy-start | bytes 3076
  150.5 15.3 %all-to-all-start = ((s32[32,2,576]{2,1,0:T(2,128)}), s32[32,2,576]{2,1,0:T(2,128)S(1)}, u32[]{:S(2)}, u32[]{:S(2)}) async-start(s32[32,2,576]{2,1,0:T(2,128)} %sub.59), calls=%async_computation | async-start | bytes 327680 | tf_op jit(solution)/shard_map/all_to_all | solution.py:56
  157.8 226.5 %reduce-scatter.2.cloned.1.call-start = ((), (), s32[]{:S(2)}) async-start(), calls=%async_computation.2 | async-start | bytes 1179648 | tf_op jit(solution)/shard_map/reduce_scatter | solution.py:88
  300.0 12.2 %copy-start = (s32[1024]{0:T(1024)S(1)}, s32[1024]{0:T(1024)}, u32[]{:S(2)}) copy-start(s32[1024]{0:T(1024)} %iota_add_fusion.1) | copy-start | bytes 12292
  300.0 12.2 %copy-start.3 = (s32[128]{0:T(128)S(1)}, s32[128]{0:T(128)}, u32[]{:S(2)}) copy-start(s32[128]{0:T(128)} %slice_bitcast_fusion) | copy-start | bytes 1540
  312.2 9.2 %copy-start.2 = (s32[2,128]{1,0:T(2,128)S(1)}, s32[2,128]{1,0:T(2,128)}, u32[]{:S(2)}) copy-start(s32[2,128]{1,0:T(2,128)} %param.10) | copy-start | bytes 3076
  312.2 85.3 %copy-start.4 = (s32[16]{0:T(128)S(1)}, s32[16]{0:T(128)}, u32[]{:S(2)}) copy-start(s32[16]{0:T(128)} %param.11) | copy-start | bytes 196
Sparse Core Ops, SparseCore 0:
  321.5 62.8 reduce-scatter.1
where the time goes:
time: 409 us; the launch traced here: 405 us
  matrix products  159 us (39%)
  local copies, waits for them, and re-layouts  107 us (26%)
  waiting for transfers between devices  69.5 us (17%)
  other arithmetic  41.8 us (10%)
  between operations  14.2 us (3%)
  starting transfers between devices  7.55 us (2%)
  blocking collectives  5.67 us (1%)
    dot_general x2, matrix products, add_group(): jnp.dot(row_hot, col_hot, preferred_element_type=jnp.float32)  119 us
    reduce_scatter x1, waiting for transfers between devices, per_device(): lax.psum_scatter(lax.dot_general(selector, updated, (((1,), (1,)), ((), (...  62.9 us
    gather x1, local copies, waits for them, and re-layouts, per_device(): first_label = labels[edge_tiles[:, 0, :].reshape(-1)]  52.1 us
    gather x1, local copies, waits for them, and re-layouts, per_device(): second_label = labels[edge_tiles[:, 1, :].reshape(-1)]  52.1 us
    dot_general x1, matrix products, per_device(): lax.dot_general(owner_match.astype(jnp.float32), carried, (((0,), (0,)),...  22.8 us
    dot_general x2, other arithmetic, add_group(): jnp.dot(row_hot, col_hot, preferred_element_type=jnp.float32)  14.1 us
    mul x1, other arithmetic, per_device(): slot_hot * row_value[:, None]  12.6 us
    add x1, other arithmetic, per_device(): updated = counts + increments  12.2 us
  transfers between devices with their start and end apart: 2, of which 2 were waited for; matrix products, arithmetic and copies ran while one was open for 0% of the time, Pallas kernels for 0%

commit v1 on v0

v1 whole, which is shorter than its diff:
```python
import functools

import jax
import jax.numpy as jnp
from jax import lax
from jax.experimental import pallas as pl
from jax.experimental.pallas import tpu as pltpu
from jax.sharding import PartitionSpec as P

COPIES = 4


def entropy_term(value):
    return value * jnp.log(jnp.maximum(value, 1.0))


def log2_of(size):
    assert size & (size - 1) == 0
    return size.bit_length() - 1


def ingest_kernel(
    rows_shift, cols_shift, col_shift, devices, ids_smem, ids_ref, table_ref, out_ref, picked, labs, placed
):
    blocks = ids_ref.shape[0]
    slots = placed.shape[0]
    rows_mask = (1 << rows_shift) - 1
    cols_mask = (1 << cols_shift) - 1

    @pl.loop(0, blocks)
    def _(block):
        for lane in range(128):
            line = lax.shift_right_logical(ids_smem[block, lane], 7)
            picked[pl.ds(block * 128 + lane, 1), :] = table_ref[pl.ds(line, 1), :]

    sublane = lax.broadcasted_iota(jnp.int32, (128, 128), 0)

    @pl.loop(0, blocks // 4)
    def _(four):
        for step in range(4):
            block = four * 4 + step
            lines = picked[pl.ds(pl.multiple_of(block * 128, 128), 128), :].T
            lane = ids_ref[pl.ds(block, 1), :] & 127
            labs[pl.ds(block, 1), :] = jnp.sum(
                jnp.where(sublane == lane, lines, 0), axis=0, keepdims=True
            )

    placed[...] = jnp.zeros_like(placed)
    depth = lax.broadcasted_iota(jnp.int32, (128, 256), 0)
    width = lax.broadcasted_iota(jnp.int32, (128, 256), 1)
    upto = jnp.where((depth <= width) | (width >= 128), 1.0, 0.0).astype(jnp.bfloat16)
    owner_ids = lax.broadcasted_iota(jnp.int32, (devices, 128), 0)
    slot_ids = lax.broadcasted_iota(jnp.int32, (slots, 128), 0)
    group = 8

    def place(index, carry):
        row = labs[pl.ds(pl.multiple_of(index * group, group), group), :]
        col = jnp.concatenate([row[k ^ 1 : (k ^ 1) + 1, :] for k in range(group)], axis=0)
        owner = ((row >> rows_shift) << col_shift) + (col >> cols_shift)
        hot = [owner_ids == owner[k : k + 1, :] for k in range(group)]
        counted = jnp.dot(
            jnp.concatenate([jnp.where(h, 1.0, 0.0).astype(jnp.bfloat16) for h in hot], axis=0),
            upto,
            preferred_element_type=jnp.float32,
        )
        row_value = (row & rows_mask) + 1
        col_value = (col & cols_mask) + 1
        digits = [
            digit.astype(jnp.float32)
            for digit in (row_value >> 6, row_value & 63, col_value >> 6, col_value & 63)
        ]
        slot_parts = []
        digit_parts = []
        for k in range(group):
            part = counted[k * devices : (k + 1) * devices, :]
            rank = jnp.sum(jnp.where(hot[k], part[:, :128] + carry, 0.0), axis=0, keepdims=True)
            carry = carry + part[:, 128:]
            slot_parts.append(
                jnp.where(slot_ids == rank.astype(jnp.int32) - 1, 1.0, 0.0).astype(jnp.bfloat16)
            )
            digit_parts.append(
                jnp.concatenate(
                    [jnp.where(hot[k], d[k : k + 1, :], 0.0).astype(jnp.bfloat16) for d in digits],
                    axis=0,
                )
            )
        placed[...] += lax.dot_general(
            jnp.concatenate(slot_parts, axis=1),
            jnp.concatenate(digit_parts, axis=1),
            (((1,), (1,)), ((), ())),
            preferred_element_type=jnp.float32,
        )
        return carry

    lax.fori_loop(0, blocks // group, place, jnp.zeros((devices, 128), jnp.float32))
    flat = placed[...].T.astype(jnp.int32)
    out_ref[:, 0, :] = flat[:devices] * 64 + flat[devices : 2 * devices] - 1
    out_ref[:, 1, :] = flat[2 * devices : 3 * devices] * 64 + flat[3 * devices :] - 1


def ingest(labels, edge_tiles, rows_tile, cols_tile, col_devices, devices, slots):
    ids = edge_tiles.reshape(-1, 128)
    blocks = ids.shape[0]
    return pl.pallas_call(
        functools.partial(
            ingest_kernel, log2_of(rows_tile), log2_of(cols_tile), log2_of(col_devices), devices
        ),
        out_shape=jax.ShapeDtypeStruct((devices, 2, slots), jnp.int32),
        in_specs=[
            pl.BlockSpec(memory_space=pltpu.SMEM),
            pl.BlockSpec(memory_space=pltpu.VMEM),
            pl.BlockSpec(memory_space=pltpu.VMEM),
        ],
        out_specs=pl.BlockSpec(memory_space=pltpu.VMEM),
        scratch_shapes=[
            pltpu.VMEM((blocks * 128, 128), jnp.int32),
            pltpu.VMEM((blocks, 128), jnp.int32),
            pltpu.VMEM((slots, 4 * devices), jnp.float32),
        ],
        name="ingest",
    )(ids, ids, labels.reshape(-1, 128))


def scatter_kernel(
    capacity, cols_tiles, words, proposals, counts, out, source_rows, target_rows, copies, main, sem_in, sem_out
):
    total = counts.shape[0]
    arrive = pltpu.make_async_copy(counts, main.at[pl.ds(0, total)], sem_in)
    arrive.start()
    zeros = jnp.zeros((128, 128), jnp.float32)
    for copy in copies:

        @pl.loop(0, total // 128)
        def _(i):
            copy[pl.ds(pl.multiple_of(i * 128, 128), 128), :] = zeros

    arrive.wait()
    lanes = lax.broadcasted_iota(jnp.int32, (1, 128), 1)
    sums = (main,) + tuple(copies)

    @pl.loop(0, words.shape[0])
    def _(sender):
        for slot in range(capacity):
            word = words[sender, slot]
            line = pl.ds(lax.shift_right_logical(word, 7), 1)
            hot = (jnp.full((1, 128), word, jnp.int32) & 127) == lanes
            sums[slot % len(sums)][line, :] += jnp.where(hot, 1.0, 0.0)

    chunk = total // 8
    for n in range(8):

        @pl.loop(0, chunk // 64)
        def _(i):
            at = pl.ds(pl.multiple_of(n * chunk + i * 64, 64), 64)
            value = main[at, :]
            for copy in copies:
                value = value + copy[at, :]
            main[at, :] = value

        at = pl.ds(n * chunk, chunk)
        pltpu.make_async_copy(main.at[at], out.at[at], sem_out).start()

    rows_tile = total // cols_tiles
    first = lax.axis_index("row") * rows_tile
    mine = source_rows.shape[0]
    offset = lax.axis_index("row") * mine

    def line_of(row):
        return pl.ds(((row >> 3) * cols_tiles << 3) + (row & 7), cols_tiles, stride=8)

    @pl.loop(0, mine)
    def _(p):
        source_rows[p] = main[line_of(proposals[0, offset + p] - first), :]

    @pl.loop(0, target_rows.shape[0])
    def _(p):
        row = proposals[1, p] - first
        here = (row >= 0) & (row < rows_tile)
        value = main[line_of(jnp.where(here, row, 0)), :]
        target_rows[p] = value * jnp.where(here, 1.0, 0.0)

    pltpu.make_async_copy(main.at[pl.ds(0, total)], out, sem_out).wait()


def scatter(counts, words, proposals, capacity, row_devices):
    rows_tile, cols_tile = counts.shape
    cols_tiles = cols_tile // 128
    lines = counts.reshape(rows_tile // 8, 8, cols_tiles, 128).transpose(0, 2, 1, 3).reshape(-1, 128)
    total = lines.shape[0]
    count = proposals.shape[1]
    out, source_rows, target_rows = pl.pallas_call(
        functools.partial(scatter_kernel, capacity, cols_tiles),
        out_shape=(
            jax.ShapeDtypeStruct(lines.shape, jnp.float32),
            jax.ShapeDtypeStruct((count // row_devices, cols_tiles, 128), jnp.float32),
            jax.ShapeDtypeStruct((count, cols_tiles, 128), jnp.float32),
        ),
        in_specs=[
            pl.BlockSpec(memory_space=pltpu.SMEM),
            pl.BlockSpec(memory_space=pltpu.SMEM),
            pl.BlockSpec(memory_space=pl.ANY),
        ],
        out_specs=(
            pl.BlockSpec(memory_space=pl.ANY),
            pl.BlockSpec(memory_space=pltpu.VMEM),
            pl.BlockSpec(memory_space=pltpu.VMEM),
        ),
        scratch_shapes=[
            tuple(pltpu.VMEM((total + 8, 128), jnp.float32) for _ in range(COPIES - 1)),
            pltpu.VMEM((total + 8, 128), jnp.float32),
            pltpu.SemaphoreType.DMA,
            pltpu.SemaphoreType.DMA,
        ],
        compiler_params=pltpu.CompilerParams(vmem_limit_bytes=60000000),
        name="scatter",
    )(words, proposals, lines)
    updated = out.reshape(rows_tile // 8, cols_tiles, 8, 128).transpose(0, 2, 1, 3).reshape(rows_tile, cols_tile)
    return updated, source_rows, target_rows


def per_device(counts, labels, edge_tiles, proposals, accept_flags):
    rows_tile, cols_tile = counts.shape
    row_devices = lax.axis_size("row")
    col_devices = lax.axis_size("col")
    devices = row_devices * col_devices
    edge_count = edge_tiles.shape[0] * edge_tiles.shape[2]
    capacity = 9 * edge_count // (2 * devices)
    slots = -(-capacity // 128) * 128
    outgoing = ingest(labels, edge_tiles, rows_tile, cols_tile, col_devices, devices, slots)
    arrived = lax.all_to_all(outgoing, ("row", "col"), split_axis=0, concat_axis=0, tiled=True)
    row, col = arrived[:, 0, :], arrived[:, 1, :]
    line = (((row >> 3) * (cols_tile // 128) + (col >> 7)) << 3) + (row & 7)
    words = jnp.where(row >= 0, (line << 7) + (col & 127), rows_tile * cols_tile)
    updated, own, targets = scatter(counts, words, proposals, capacity, row_devices)

    proposal_count = proposals.shape[1]
    mine = proposal_count // row_devices
    row_index = lax.axis_index("row")
    col_index = lax.axis_index("col")
    other = jnp.sum(
        lax.all_to_all(
            targets.reshape((row_devices, mine) + targets.shape[1:]), "row", split_axis=0, concat_axis=0, tiled=True
        ),
        axis=0,
    )
    pairs = lax.dynamic_slice_in_dim(proposals, row_index * mine, mine, 1)
    position = (
        col_index * cols_tile
        + 128 * lax.broadcasted_iota(jnp.int32, own.shape, 1)
        + lax.broadcasted_iota(jnp.int32, own.shape, 2)
    )
    at_source = position == pairs[0][:, None, None]
    at_target = position == pairs[1][:, None, None]
    mixed = entropy_term(own + other) - entropy_term(own) - entropy_term(other)
    zero = jnp.float32(0.0)
    parts = jnp.stack(
        [
            jnp.sum(jnp.where(at_source | at_target, zero, mixed), axis=(1, 2)),
            jnp.sum(jnp.where(at_source, own, zero), axis=(1, 2)),
            jnp.sum(jnp.where(at_source, other, zero), axis=(1, 2)),
            jnp.sum(jnp.where(at_target, other, zero), axis=(1, 2)),
            jnp.sum(own, axis=(1, 2)),
            jnp.sum(other, axis=(1, 2)),
        ]
    )
    spread = lax.dynamic_update_slice(
        jnp.zeros((parts.shape[0], proposal_count), jnp.float32), parts, (0, row_index * mine)
    )
    per_col = accept_flags.shape[0]
    sums = lax.dynamic_slice_in_dim(lax.psum(spread, ("row", "col")), col_index * per_col, per_col, 1)
    pair_sum, self_source, cross_count, self_target, degree_source, degree_target = sums
    corner = (
        entropy_term(self_source + 2.0 * cross_count + self_target)
        - entropy_term(self_source)
        - entropy_term(self_target)
        - 2.0 * entropy_term(cross_count)
    )
    change = (
        -(pair_sum + 0.5 * corner)
        + entropy_term(degree_source + degree_target)
        - entropy_term(degree_source)
        - entropy_term(degree_target)
    )
    merge_cost = change / (rows_tile * row_devices)
    accepted_cost = jnp.where(accept_flags == 1, merge_cost, zero)
    return (updated, merge_cost, accepted_cost)


def solution(mesh):
    return jax.shard_map(
        per_device,
        mesh=mesh,
        in_specs=(P("row", "col"), P(), P(("row", "col"), None, None), P(), P("col")),
        out_specs=(P("row", "col"), P("col"), P("col")),
        check_vma=False,
    )
```

time: 409 us -> 133 us (0.33)
  matrix products: 159 us -> 0 us
  local copies, waits for them, and re-layouts: 107 us -> 0.52 us
  Pallas kernels: 0 us -> 61.2 us
  waiting for transfers between devices: 69.5 us -> 16.7 us
  other arithmetic: 41.8 us -> 3.38 us
  blocking collectives: 5.67 us -> 38.3 us
  between operations: 14.2 us -> 0.72 us
    dot_general x6 -> x0, matrix products: 159 us -> none  [the longest x2 119 us: add_group(): jnp.dot(row_hot, col_hot, preferred_element_type=jnp.float32)]
    gather x2 -> x0, local copies, waits for them, and re-layouts: 104 us -> none  [the longest x1 52.1 us: per_device(): first_label = labels[edge_tiles[:, 0, :].reshape(-1)]]
    reduce_scatter x1 -> x0, waiting for transfers between devices: 62.9 us -> none  [per_device(): lax.psum_scatter(lax.dot_general(selector, updated, (((1,), (1,)), ((), (...]
    pallas_call x0 -> x2, Pallas kernels: none -> 61.2 us  [the longest x1 41.6 us: scatter(): pl.pallas_call(functools.partial(scatter_kernel, capacity, cols_tiles), o...]
    psum x1, blocking collectives: 5.67 us -> 38.3 us  [per_device(): lax.psum(spread, ('row', 'col'))]
    dot_general x2 -> x0, other arithmetic: 14.1 us -> none  [add_group(): jnp.dot(row_hot, col_hot, preferred_element_type=jnp.float32)]
    add x5 -> x1, other arithmetic: 12.9 us -> 0.01 us  [per_device(): col_index * cols_tile + 128 * lax.broadcasted_iota(jnp.int32, own.shape, 1)]
    mul x1 -> x0, other arithmetic: 12.6 us -> none  [per_device(): slot_hot * row_value[:, None]]
where the time goes in v1:
time: 133 us; the launch traced here: 132 us
  Pallas kernels  61.2 us (46%)
  blocking collectives  38.3 us (29%)
  waiting for transfers between devices  16.7 us (13%)
  starting transfers between devices  10.8 us (8%)
  other arithmetic  3.38 us (3%)
    pallas_call x1, Pallas kernels, scatter(): pl.pallas_call(functools.partial(scatter_kernel, capacity, cols_tiles), o...  41.6 us
    psum x1, blocking collectives, per_device(): lax.psum(spread, ('row', 'col'))  38.3 us
    pallas_call x1, Pallas kernels, ingest(): pl.pallas_call(functools.partial(ingest_kernel, log2_of(rows_tile), log2_...  19.5 us
    all_to_all x1, waiting for transfers between devices, per_device(): lax.all_to_all(targets.reshape((row_devices, mine) + targets.shape[1:]),...  8.67 us
    all_to_all x1, waiting for transfers between devices, per_device(): lax.all_to_all(outgoing, ('row', 'col'), split_axis=0, concat_axis=0, til...  7.99 us
    all_to_all x1, starting transfers between devices, per_device(): lax.all_to_all(outgoing, ('row', 'col'), split_axis=0, concat_axis=0, til...  7.32 us
    all_to_all x1, starting transfers between devices, per_device(): lax.all_to_all(targets.reshape((row_devices, mine) + targets.shape[1:]),...  3.48 us
  transfers between devices with their start and end apart: 2, of which 2 were waited for; matrix products, arithmetic and copies ran while one was open for 0% of the time, Pallas kernels for 0%

profile of v1, /device:TPU:0, one launch (start us, length us, event | category | flops | bytes accessed | tf_op | source)
XLA Modules:
  0.0 131.6 jit_solution(13743811837765989564)
XLA Ops:
  0.6 0.0 copy-start
  0.6 0.0 copy-start.1
  0.7 19.5 %ingest.1 = s32[32,2,640]{2,1,0:T(2,128)} custom-call(s32[64,128]{1,0:T(8,128)} %bitcast.132, s32[64,128]{1,0:T(8,128)} %bitcast.133, s32[7680,128]{1,0:T(8,128)} %bitcast.130), custom_call_target="tpu_custom_call" | custom-call | tf_op jit(solution)/shard_map/ingest/pallas_call | solution.py:104
  20.2 7.3 %all-to-all-start = ((s32[32,2,640]{2,1,0:T(2,128)}), s32[32,2,640]{2,1,0:T(2,128)S(1)}, u32[]{:S(2)}, u32[]{:S(2)}) async-start(s32[32,2,640]{2,1,0:T(2,128)} %ingest.1), calls=%async_computation | async-start | bytes 327680 | tf_op jit(solution)/shard_map/all_to_all | solution.py:230
  27.5 8.0 %all-to-all-done = s32[32,2,640]{2,1,0:T(2,128)S(1)} async-done(((s32[32,2,640]{2,1,0:T(2,128)}), s32[32,2,640]{2,1,0:T(2,128)S(1)}, u32[]{:S(2)}, u32[]{:S(2)}) %all-to-all-start) | async-done | bytes 163872 | tf_op jit(solution)/shard_map/all_to_all | solution.py:230
  35.5 0.1 fusion.20
  35.7 0.7 select_bitcast_fusion.words
  36.3 41.6 %scatter.1 = (f32[16384,128]{1,0:T(8,128)}, f32[32,8,128]{2,1,0:T(8,128)}, f32[128,8,128]{2,1,0:T(8,128)}) custom-call(s32[32,640]{1,0:T(8,128)} %select_bitcast_fusion.words, s32[2,128]{1,0:T(2,128)} %proposals.1, f32[16384,128]{1,0:T(8,128)} %bitcast.129), custom_call_target="tpu_custom_call" | custom-call | tf_op jit(solution)/shard_map/scatter/pallas_call | solution.py:191
  78.0 3.5 %all-to-all-start.1 = ((f32[4,32,8,128]{3,2,1,0:T(8,128)}), f32[4,32,8,128]{3,2,1,0:T(8,128)S(1)}, u32[]{:S(2)}, u32[]{:S(2)}) async-start(f32[4,32,8,128]{3,2,1,0:T(8,128)} %bitcast.131), calls=%async_computation.1 | async-start | bytes 1048576 | tf_op jit(solution)/shard_map/all_to_all | solution.py:241
  81.5 0.0 copy-done
  81.5 0.1 constant_dynamic-slice_fusion.1
  81.6 8.7 %all-to-all-done.1 = f32[4,32,8,128]{3,2,1,0:T(8,128)S(1)} async-done(((f32[4,32,8,128]{3,2,1,0:T(8,128)}), f32[4,32,8,128]{3,2,1,0:T(8,128)S(1)}, u32[]{:S(2)}, u32[]{:S(2)}) %all-to-all-start.1) | async-done | bytes 524320 | tf_op jit(solution)/shard_map/all_to_all | solution.py:241
  90.2 0.3 fusion.18
  90.6 1.9 %select_reduce_fusion = (f32[32]{0:T(128)S(1)}, f32[32]{0:T(128)S(1)}, f32[32]{0:T(128)S(1)}, f32[32]{0:T(128)S(1)}, f32[32]{0:T(128)S(1)}) fusion(f32[32,8,128]{2,1,0:T(8,128)S(1)} %get-tuple-element.10, s32[32]{0:T(128)S(1)} %get-tuple-element.21, s32[8]{0:T(128)S(1)} %multiply_add_fusion, f32[32,8,128]{2,1,0:T(8,128)} %get-tuple-element.7, ...), kind=kLoop, calls=%fused_computation | loop fusion | flops 720736 | bytes 263072 | tf_op jit(solution)/shard_map/reduce_sum | solution.py:261
  92.5 0.2 dynamic_update_slice.3
  92.7 38.3 %psum.7 = f32[6,128]{1,0:T(8,128)S(1)} all-reduce(f32[6,128]{1,0:T(8,128)S(1)} %dynamic_update_slice.3), channel_id=1, replica_groups=mesh['row'=4,'col'=8] {'row','col'}, use_global_device_ids=true, to_apply=%region_7.8 | all-reduce | flops 768 | bytes 6144 | tf_op jit(solution)/shard_map/psum | solution.py:270
  131.0 0.1 constant_dynamic-slice_fusion
  131.0 0.0 copy-done.1
  131.0 0.5 compare_select_fusion
  (4 shorter events, 0.0 us)
Async XLA Ops:
  0.6 80.8 %copy-start = (s32[2,128]{1,0:T(2,128)S(1)}, s32[2,128]{1,0:T(2,128)}, u32[]{:S(2)}) copy-start(s32[2,128]{1,0:T(2,128)} %proposals.1) | copy-start | bytes 3076
  0.6 130.4 %copy-start.1 = (s32[16]{0:T(128)S(1)}, s32[16]{0:T(128)}, u32[]{:S(2)}) copy-start(s32[16]{0:T(128)} %param.9) | copy-start | bytes 196
  20.2 15.3 %all-to-all-start = ((s32[32,2,640]{2,1,0:T(2,128)}), s32[32,2,640]{2,1,0:T(2,128)S(1)}, u32[]{:S(2)}, u32[]{:S(2)}) async-start(s32[32,2,640]{2,1,0:T(2,128)} %ingest.1), calls=%async_computation | async-start | bytes 327680 | tf_op jit(solution)/shard_map/all_to_all | solution.py:230
  78.0 12.3 %all-to-all-start.1 = ((f32[4,32,8,128]{3,2,1,0:T(8,128)}), f32[4,32,8,128]{3,2,1,0:T(8,128)S(1)}, u32[]{:S(2)}, u32[]{:S(2)}) async-start(f32[4,32,8,128]{3,2,1,0:T(8,128)} %bitcast.131), calls=%async_computation.1 | async-start | bytes 1048576 | tf_op jit(solution)/shard_map/all_to_all | solution.py:241

commit v2 on v1

--- a/solution.py
+++ b/solution.py
@@ -237,12 +237,17 @@
     mine = proposal_count // row_devices
     row_index = lax.axis_index("row")
     col_index = lax.axis_index("col")
-    other = jnp.sum(
-        lax.all_to_all(
-            targets.reshape((row_devices, mine) + targets.shape[1:]), "row", split_axis=0, concat_axis=0, tiled=True
-        ),
-        axis=0,
-    )
+    other = targets.reshape((row_devices, mine) + targets.shape[1:])
+    for bit in range(log2_of(row_devices)):
+        halves = other.reshape((-1, 2) + other.shape[1:])
+        side = (row_index >> bit) & 1
+        swapped = lax.ppermute(
+            lax.dynamic_index_in_dim(halves, 1 - side, 1, keepdims=False),
+            "row",
+            [(device, device ^ (1 << bit)) for device in range(row_devices)],
+        )
+        other = lax.dynamic_index_in_dim(halves, side, 1, keepdims=False) + swapped
+    other = other[0]
     pairs = lax.dynamic_slice_in_dim(proposals, row_index * mine, mine, 1)
     position = (
         col_index * cols_tile
@@ -263,11 +268,17 @@
             jnp.sum(other, axis=(1, 2)),
         ]
     )
-    spread = lax.dynamic_update_slice(
-        jnp.zeros((parts.shape[0], proposal_count), jnp.float32), parts, (0, row_index * mine)
-    )
     per_col = accept_flags.shape[0]
-    sums = lax.dynamic_slice_in_dim(lax.psum(spread, ("row", "col")), col_index * per_col, per_col, 1)
+    width = -(-parts.shape[0] * per_col // 128) * 128
+    groups = mine // per_col
+    lines = parts.reshape(-1, groups, per_col).transpose(1, 0, 2).reshape(groups, -1)
+    lines = jnp.pad(lines, ((0, 0), (0, width - lines.shape[1])))
+    spread = jnp.where(
+        jnp.arange(row_devices)[:, None, None] == row_index, lines[None], zero
+    ).reshape(1, col_devices, 1, width)
+    spread = jnp.broadcast_to(spread, (row_devices, col_devices, 1, width)).reshape(devices, 1, width)
+    gathered = lax.all_to_all(spread, ("row", "col"), split_axis=0, concat_axis=0, tiled=True)
+    sums = jnp.sum(gathered, axis=(0, 1))[: parts.shape[0] * per_col].reshape(-1, per_col)
     pair_sum, self_source, cross_count, self_target, degree_source, degree_target = sums
     corner = (
         entropy_term(self_source + 2.0 * cross_count + self_target)

time: 133 us -> 102 us (0.77)
  blocking collectives: 38.3 us -> 10.1 us
  waiting for transfers between devices: 16.7 us -> 13.7 us
  local copies, waits for them, and re-layouts: 0.52 us -> 2.01 us
    psum x1 -> x0, blocking collectives: 38.3 us -> none  [per_device(): lax.psum(spread, ('row', 'col'))]
    all_to_all x0 -> x1, blocking collectives: none -> 10.1 us  [per_device(): lax.all_to_all(spread, ('row', 'col'), split_axis=0, concat_axis=0, tiled...]
    all_to_all x1 -> x0, waiting for transfers between devices: 8.67 us -> none  [per_device(): lax.all_to_all(targets.reshape((row_devices, mine) + targets.shape[1:]),...]
    ppermute x0 -> x2, waiting for transfers between devices: none -> 5.74 us  [per_device(): lax.ppermute(lax.dynamic_index_in_dim(halves, 1 - side, 1, keepdims=False...]
    all_to_all x1 -> x0, starting transfers between devices: 3.48 us -> none  [per_device(): lax.all_to_all(targets.reshape((row_devices, mine) + targets.shape[1:]),...]
    ppermute x0 -> x2, starting transfers between devices: none -> 2.59 us  [per_device(): lax.ppermute(lax.dynamic_index_in_dim(halves, 1 - side, 1, keepdims=False...]
  transfers between devices with their start and end apart: 2 -> 3, of which waited for: 2 -> 3; matrix products, arithmetic and copies ran while one was open for 0% -> 0% of each run, Pallas kernels for 0% -> 0%
where the time goes in v2:
time: 102 us; the launch traced here: 101 us
  Pallas kernels  60.1 us (59%)
  waiting for transfers between devices  13.7 us (13%)
  blocking collectives  10.1 us (10%)
  starting transfers between devices  9.91 us (10%)
  other arithmetic  4.56 us (4%)
  local copies, waits for them, and re-layouts  2.01 us (2%)
    pallas_call x1, Pallas kernels, scatter(): pl.pallas_call(functools.partial(scatter_kernel, capacity, cols_tiles), o...  40.5 us
    pallas_call x1, Pallas kernels, ingest(): pl.pallas_call(functools.partial(ingest_kernel, log2_of(rows_tile), log2_...  19.5 us
    all_to_all x1, blocking collectives, per_device(): lax.all_to_all(spread, ('row', 'col'), split_axis=0, concat_axis=0, tiled...  10.1 us
    all_to_all x1, waiting for transfers between devices, per_device(): lax.all_to_all(outgoing, ('row', 'col'), split_axis=0, concat_axis=0, til...  7.99 us
    all_to_all x1, starting transfers between devices, per_device(): lax.all_to_all(outgoing, ('row', 'col'), split_axis=0, concat_axis=0, til...  7.32 us
    ppermute x2, waiting for transfers between devices, per_device(): lax.ppermute(lax.dynamic_index_in_dim(halves, 1 - side, 1, keepdims=False...  5.74 us
    ppermute x2, starting transfers between devices, per_device(): lax.ppermute(lax.dynamic_index_in_dim(halves, 1 - side, 1, keepdims=False...  2.59 us
  transfers between devices with their start and end apart: 3, of which 3 were waited for; matrix products, arithmetic and copies ran while one was open for 0% of the time, Pallas kernels for 0%

profile of v2, /device:TPU:0, one launch (start us, length us, event | category | flops | bytes accessed | tf_op | source)
XLA Modules:
  0.0 101.1 jit_solution(5583932638251615300)
XLA Ops:
  0.7 19.5 %ingest.1 = s32[32,2,640]{2,1,0:T(2,128)} custom-call(s32[64,128]{1,0:T(8,128)} %bitcast.52, s32[64,128]{1,0:T(8,128)} %bitcast.53, s32[7680,128]{1,0:T(8,128)} %bitcast.49), custom_call_target="tpu_custom_call" | custom-call | tf_op jit(solution)/shard_map/ingest/pallas_call | solution.py:104
  20.2 7.3 %all-to-all-start = ((s32[32,2,640]{2,1,0:T(2,128)}), s32[32,2,640]{2,1,0:T(2,128)S(1)}, u32[]{:S(2)}, u32[]{:S(2)}) async-start(s32[32,2,640]{2,1,0:T(2,128)} %ingest.1), calls=%async_computation | async-start | bytes 327680 | tf_op jit(solution)/shard_map/all_to_all | solution.py:230
  27.5 8.0 %all-to-all-done = s32[32,2,640]{2,1,0:T(2,128)S(1)} async-done(((s32[32,2,640]{2,1,0:T(2,128)}), s32[32,2,640]{2,1,0:T(2,128)S(1)}, u32[]{:S(2)}, u32[]{:S(2)}) %all-to-all-start) | async-done | bytes 163872 | tf_op jit(solution)/shard_map/all_to_all | solution.py:230
  35.5 0.1 fusion.10
  35.7 0.7 select_bitcast_fusion.words
  36.3 40.5 %scatter.1 = (f32[16384,128]{1,0:T(8,128)}, f32[32,8,128]{2,1,0:T(8,128)}, f32[128,8,128]{2,1,0:T(8,128)}) custom-call(s32[32,640]{1,0:T(8,128)} %select_bitcast_fusion.words, s32[2,128]{1,0:T(2,128)} %proposals.1, f32[16384,128]{1,0:T(8,128)} %bitcast.48), custom_call_target="tpu_custom_call" | custom-call | tf_op jit(solution)/shard_map/scatter/pallas_call | solution.py:191
  76.8 1.0 dynamic-slice_bitcast_fusion
  77.8 1.6 %collective-permute-start = (f32[2,32,8,128]{3,2,1,0:T(8,128)S(1)}, f32[2,32,8,128]{3,2,1,0:T(8,128)S(1)}, u32[]{:S(2)}, u32[]{:S(2)}) collective-permute-start(f32[2,32,8,128]{3,2,1,0:T(8,128)S(1)} %dynamic-slice_bitcast_fusion), channel_id=1, source_target_pairs={{0,8},{8,0},{16,24},{24,16},{1,9},{9,1},{17,25},{25,17},{2,10},{10... | collective-permute-start | bytes 786440 | tf_op jit(solution)/shard_map/ppermute | solution.py:244
  79.5 1.1 %collective-permute-done = f32[2,32,8,128]{3,2,1,0:T(8,128)S(1)} collective-permute-done((f32[2,32,8,128]{3,2,1,0:T(8,128)S(1)}, f32[2,32,8,128]{3,2,1,0:T(8,128)S(1)}, u32[]{:S(2)}, u32[]{:S(2)}) %collective-permute-start) | collective-permute-done | bytes 262176 | tf_op jit(solution)/shard_map/ppermute | solution.py:244
  80.6 1.0 bitcast_add_fusion
  81.6 1.0 collective-permute-start.1
  82.7 0.1 broadcast_in_dim.53
  82.8 4.7 %collective-permute-done.1 = f32[1,32,8,128]{3,2,1,0:T(8,128)S(1)} collective-permute-done((f32[1,32,8,128]{3,2,1,0:T(8,128)S(1)}, f32[1,32,8,128]{3,2,1,0:T(8,128)S(1)}, u32[]{:S(2)}, u32[]{:S(2)}) %collective-permute-start.1) | collective-permute-done | bytes 131104 | tf_op jit(solution)/shard_map/ppermute | solution.py:244
  87.4 0.3 fusion.9
  87.8 1.9 %fusion.5 = (f32[32]{0:T(128)S(1)}, f32[32]{0:T(128)S(1)}, f32[32]{0:T(128)S(1)}, f32[32]{0:T(128)S(1)}, f32[32]{0:T(128)S(1)}) fusion(f32[1,32,8,128]{3,2,1,0:T(8,128)S(1)} %get-tuple-element.17, s32[32]{0:T(128)S(1)} %get-tuple-element.21, s32[8]{0:T(128)S(1)} %multiply_add_fusion, f32[32,8,128]{2,1,0:T(8,128)} %get-tuple-element.7, ...), kind=kLoop, calls=%fused_computation.12 | loop fusion | flops 720736 | bytes 263072 | tf_op jit(solution)/shard_map/reduce_sum | solution.py:266
  89.6 0.1 stack.21
  89.7 0.1 stack.22
  89.8 0.1 stack.23
  89.9 0.1 stack.24
  89.9 0.1 stack.25
  90.0 0.1 stack.26
  90.2 0.1 reshape.108
  90.3 10.1 %all_to_all.10 = f32[32,1,128]{2,1,0:T(1,128)S(1)} all-to-all(f32[32,1,128]{2,1,0:T(1,128)S(1)} %bitcast.54), channel_id=1, replica_groups=mesh['row'=4,'col'=8] {'row','col'}, dimensions={0} | all-to-all | bytes 32768 | tf_op jit(solution)/shard_map/all_to_all | solution.py:280
  100.5 0.6 compare_select_fusion
  (22 shorter events, 0.4 us)
Async XLA Ops:
  0.6 78.8 %copy-start = (s32[2,128]{1,0:T(2,128)S(1)}, s32[2,128]{1,0:T(2,128)}, u32[]{:S(2)}) copy-start(s32[2,128]{1,0:T(2,128)} %proposals.1) | copy-start | bytes 3076
  0.6 99.8 %copy-start.1 = (s32[16]{0:T(128)S(1)}, s32[16]{0:T(128)}, u32[]{:S(2)}) copy-start(s32[16]{0:T(128)} %param.9) | copy-start | bytes 196
  20.2 15.3 %all-to-all-start = ((s32[32,2,640]{2,1,0:T(2,128)}), s32[32,2,640]{2,1,0:T(2,128)S(1)}, u32[]{:S(2)}, u32[]{:S(2)}) async-start(s32[32,2,640]{2,1,0:T(2,128)} %ingest.1), calls=%async_computation | async-start | bytes 327680 | tf_op jit(solution)/shard_map/all_to_all | solution.py:230
  77.8 2.7 %collective-permute-start = (f32[2,32,8,128]{3,2,1,0:T(8,128)S(1)}, f32[2,32,8,128]{3,2,1,0:T(8,128)S(1)}, u32[]{:S(2)}, u32[]{:S(2)}) collective-permute-start(f32[2,32,8,128]{3,2,1,0:T(8,128)S(1)} %dynamic-slice_bitcast_fusion), channel_id=1, source_target_pairs={{0,8},{8,0},{16,24},{24,16},{1,9},{9,1},{17,25},{25,17},{2,10},{10... | collective-permute-start | bytes 786440 | tf_op jit(solution)/shard_map/ppermute | solution.py:244
  81.6 5.8 %collective-permute-start.1 = (f32[1,32,8,128]{3,2,1,0:T(8,128)S(1)}, f32[1,32,8,128]{3,2,1,0:T(8,128)S(1)}, u32[]{:S(2)}, u32[]{:S(2)}) collective-permute-start(f32[1,32,8,128]{3,2,1,0:T(8,128)S(1)} %constant_dynamic-slice_fusion), channel_id=1, source_target_pairs={{0,16},{8,24},{16,0},{24,8},{1,17},{9,25},{17,1},{25,9},{2,18},{10... | collective-permute-start | bytes 393224 | tf_op jit(solution)/shard_map/ppermute | solution.py:244

commit v3 on v2

--- a/solution.py
+++ b/solution.py
@@ -7,7 +7,8 @@
 from jax.experimental.pallas import tpu as pltpu
 from jax.sharding import PartitionSpec as P
 
-COPIES = 4
+COPIES = 5
+GROUP = 4
 
 
 def entropy_term(value):
@@ -19,43 +20,42 @@
     return size.bit_length() - 1
 
 
-def ingest_kernel(
-    rows_shift, cols_shift, col_shift, devices, ids_smem, ids_ref, table_ref, out_ref, picked, labs, placed
-):
+def ingest_kernel(rows_shift, cols_shift, col_shift, devices, ids_smem, ids_ref, table_ref, out_ref, picked, placed):
     blocks = ids_ref.shape[0]
     slots = placed.shape[0]
+    group = picked.shape[0] // 128
     rows_mask = (1 << rows_shift) - 1
     cols_mask = (1 << cols_shift) - 1
 
-    @pl.loop(0, blocks)
-    def _(block):
-        for lane in range(128):
-            line = lax.shift_right_logical(ids_smem[block, lane], 7)
-            picked[pl.ds(block * 128 + lane, 1), :] = table_ref[pl.ds(line, 1), :]
-
+    def pick(index):
+        for k in range(group):
+            for lane in range(128):
+                line = lax.shift_right_logical(ids_smem[index * group + k, lane], 7)
+                picked[k * 128 + lane : k * 128 + lane + 1, :] = table_ref[pl.ds(line, 1), :]
+
+    placed[...] = jnp.zeros_like(placed)
     sublane = lax.broadcasted_iota(jnp.int32, (128, 128), 0)
-
-    @pl.loop(0, blocks // 4)
-    def _(four):
-        for step in range(4):
-            block = four * 4 + step
-            lines = picked[pl.ds(pl.multiple_of(block * 128, 128), 128), :].T
-            lane = ids_ref[pl.ds(block, 1), :] & 127
-            labs[pl.ds(block, 1), :] = jnp.sum(
-                jnp.where(sublane == lane, lines, 0), axis=0, keepdims=True
-            )
-
-    placed[...] = jnp.zeros_like(placed)
     depth = lax.broadcasted_iota(jnp.int32, (128, 256), 0)
     width = lax.broadcasted_iota(jnp.int32, (128, 256), 1)
     upto = jnp.where((depth <= width) | (width >= 128), 1.0, 0.0).astype(jnp.bfloat16)
     owner_ids = lax.broadcasted_iota(jnp.int32, (devices, 128), 0)
     slot_ids = lax.broadcasted_iota(jnp.int32, (slots, 128), 0)
-    group = 8
+    steps = blocks // group
+    pick(0)
 
     def place(index, carry):
-        row = labs[pl.ds(pl.multiple_of(index * group, group), group), :]
-        col = jnp.concatenate([row[k ^ 1 : (k ^ 1) + 1, :] for k in range(group)], axis=0)
+        turned = [picked[k * 128 : (k + 1) * 128, :].T for k in range(group)]
+        pick(jnp.minimum(index + 1, steps - 1))
+        label = [
+            jnp.sum(
+                jnp.where(sublane == (ids_ref[pl.ds(index * group + k, 1), :] & 127), turned[k], 0),
+                axis=0,
+                keepdims=True,
+            )
+            for k in range(group)
+        ]
+        row = jnp.concatenate(label, axis=0)
+        col = jnp.concatenate([label[k ^ 1] for k in range(group)], axis=0)
         owner = ((row >> rows_shift) << col_shift) + (col >> cols_shift)
         hot = [owner_ids == owner[k : k + 1, :] for k in range(group)]
         counted = jnp.dot(
@@ -92,7 +92,7 @@
         )
         return carry
 
-    lax.fori_loop(0, blocks // group, place, jnp.zeros((devices, 128), jnp.float32))
+    lax.fori_loop(0, steps, place, jnp.zeros((devices, 128), jnp.float32))
     flat = placed[...].T.astype(jnp.int32)
     out_ref[:, 0, :] = flat[:devices] * 64 + flat[devices : 2 * devices] - 1
     out_ref[:, 1, :] = flat[2 * devices : 3 * devices] * 64 + flat[3 * devices :] - 1
@@ -100,7 +100,6 @@
 
 def ingest(labels, edge_tiles, rows_tile, cols_tile, col_devices, devices, slots):
     ids = edge_tiles.reshape(-1, 128)
-    blocks = ids.shape[0]
     return pl.pallas_call(
         functools.partial(
             ingest_kernel, log2_of(rows_tile), log2_of(cols_tile), log2_of(col_devices), devices
@@ -113,8 +112,7 @@
         ],
         out_specs=pl.BlockSpec(memory_space=pltpu.VMEM),
         scratch_shapes=[
-            pltpu.VMEM((blocks * 128, 128), jnp.int32),
-            pltpu.VMEM((blocks, 128), jnp.int32),
+            pltpu.VMEM((GROUP * 128, 128), jnp.int32),
             pltpu.VMEM((slots, 4 * devices), jnp.float32),
         ],
         name="ingest",
@@ -122,29 +120,58 @@
 
 
 def scatter_kernel(
-    capacity, cols_tiles, words, proposals, counts, out, source_rows, target_rows, copies, main, sem_in, sem_out
+    capacity,
+    cols_tiles,
+    words_hbm,
+    proposals,
+    counts,
+    out,
+    source_rows,
+    target_rows,
+    copies,
+    main,
+    words,
+    sem_in,
+    sem_words,
+    sem_out,
 ):
     total = counts.shape[0]
     arrive = pltpu.make_async_copy(counts, main.at[pl.ds(0, total)], sem_in)
     arrive.start()
-    zeros = jnp.zeros((128, 128), jnp.float32)
+    listed = pltpu.make_async_copy(words_hbm, words, sem_words)
+    listed.start()
+    zeros = jnp.zeros((256, 128), jnp.float32)
     for copy in copies:
 
-        @pl.loop(0, total // 128)
+        @pl.loop(0, total // 256)
         def _(i):
-            copy[pl.ds(pl.multiple_of(i * 128, 128), 128), :] = zeros
-
+            copy[pl.ds(pl.multiple_of(i * 256, 256), 256), :] = zeros
+
+    listed.wait()
     arrive.wait()
     lanes = lax.broadcasted_iota(jnp.int32, (1, 128), 1)
     sums = (main,) + tuple(copies)
 
-    @pl.loop(0, words.shape[0])
-    def _(sender):
-        for slot in range(capacity):
-            word = words[sender, slot]
+    def add_line(at, count):
+        for slot in range(count):
+            word = words[at, slot]
             line = pl.ds(lax.shift_right_logical(word, 7), 1)
             hot = (jnp.full((1, 128), word, jnp.int32) & 127) == lanes
             sums[slot % len(sums)][line, :] += jnp.where(hot, 1.0, 0.0)
+
+    per_sender = -(-capacity // 128)
+    whole, rest = capacity // 128, capacity % 128
+
+    @pl.loop(0, words.shape[0] // per_sender)
+    def _(sender):
+        if whole:
+
+            @pl.loop(0, whole)
+            def _(part):
+                add_line(sender * per_sender + part, 128)
+
+        if rest:
+            add_line(sender * per_sender + whole, rest)
 
     chunk = total // 8
     for n in range(8):
@@ -168,11 +195,11 @@
     def line_of(row):
         return pl.ds(((row >> 3) * cols_tiles << 3) + (row & 7), cols_tiles, stride=8)
 
-    @pl.loop(0, mine)
+    @pl.loop(0, mine, unroll=8)
     def _(p):
         source_rows[p] = main[line_of(proposals[0, offset + p] - first), :]
 
-    @pl.loop(0, target_rows.shape[0])
+    @pl.loop(0, target_rows.shape[0], unroll=8)
     def _(p):
         row = proposals[1, p] - first
         here = (row >= 0) & (row < rows_tile)
@@ -196,7 +223,7 @@
             jax.ShapeDtypeStruct((count, cols_tiles, 128), jnp.float32),
         ),
         in_specs=[
-            pl.BlockSpec(memory_space=pltpu.SMEM),
+            pl.BlockSpec(memory_space=pl.ANY),
             pl.BlockSpec(memory_space=pltpu.SMEM),
             pl.BlockSpec(memory_space=pl.ANY),
         ],
@@ -208,6 +235,8 @@
         scratch_shapes=[
             tuple(pltpu.VMEM((total + 8, 128), jnp.float32) for _ in range(COPIES - 1)),
             pltpu.VMEM((total + 8, 128), jnp.float32),
+            pltpu.SMEM(words.shape, jnp.int32),
+            pltpu.SemaphoreType.DMA,
             pltpu.SemaphoreType.DMA,
             pltpu.SemaphoreType.DMA,
         ],
@@ -230,7 +259,7 @@
     arrived = lax.all_to_all(outgoing, ("row", "col"), split_axis=0, concat_axis=0, tiled=True)
     row, col = arrived[:, 0, :], arrived[:, 1, :]
     line = (((row >> 3) * (cols_tile // 128) + (col >> 7)) << 3) + (row & 7)
-    words = jnp.where(row >= 0, (line << 7) + (col & 127), rows_tile * cols_tile)
+    words = jnp.where(row >= 0, (line << 7) + (col & 127), rows_tile * cols_tile).reshape(-1, 128)
     updated, own, targets = scatter(counts, words, proposals, capacity, row_devices)
 
     proposal_count = proposals.shape[1]

time: 102 us -> 89.9 us (0.88)
  Pallas kernels: 60.1 us -> 49.4 us
  starting transfers between devices: 9.91 us -> 7.6 us
    pallas_call x1, Pallas kernels: 19.5 us -> 13.1 us  [ingest(): pl.pallas_call(functools.partial(ingest_kernel, log2_of(rows_tile), log2_...]
    pallas_call x1, Pallas kernels: 40.5 us -> 36.3 us  [scatter(): pl.pallas_call(functools.partial(scatter_kernel, capacity, cols_tiles), o...]
    ppermute x2, starting transfers between devices: 2.59 us -> 0.28 us  [per_device(): lax.ppermute(lax.dynamic_index_in_dim(halves, 1 - side, 1, keepdims=False...]
where the time goes in v3:
time: 89.9 us; the launch traced here: 89.3 us
  Pallas kernels  49.4 us (55%)
  waiting for transfers between devices  14.7 us (16%)
  blocking collectives  10.3 us (11%)
  starting transfers between devices  7.6 us (8%)
  other arithmetic  4.82 us (5%)
  local copies, waits for them, and re-layouts  1.88 us (2%)
    pallas_call x1, Pallas kernels, scatter(): pl.pallas_call(functools.partial(scatter_kernel, capacity, cols_tiles), o...  36.3 us
    pallas_call x1, Pallas kernels, ingest(): pl.pallas_call(functools.partial(ingest_kernel, log2_of(rows_tile), log2_...  13.1 us
    all_to_all x1, blocking collectives, per_device(): lax.all_to_all(spread, ('row', 'col'), split_axis=0, concat_axis=0, tiled...  10.3 us
    all_to_all x1, waiting for transfers between devices, per_device(): lax.all_to_all(outgoing, ('row', 'col'), split_axis=0, concat_axis=0, til...  7.99 us
    all_to_all x1, starting transfers between devices, per_device(): lax.all_to_all(outgoing, ('row', 'col'), split_axis=0, concat_axis=0, til...  7.32 us
    ppermute x2, waiting for transfers between devices, per_device(): lax.ppermute(lax.dynamic_index_in_dim(halves, 1 - side, 1, keepdims=False...  6.67 us
    reduce_sum x1, other arithmetic, per_device(): jnp.sum(jnp.where(at_target, other, zero), axis=(1, 2))  1.86 us
  transfers between devices with their start and end apart: 3, of which 3 were waited for; matrix products, arithmetic and copies ran while one was open for 0% of the time, Pallas kernels for 0%

profile of v3, /device:TPU:0, one launch (start us, length us, event | category | flops | bytes accessed | tf_op | source)
XLA Modules:
  0.0 89.3 jit_solution(7121499903722624311)
XLA Ops:
  0.7 13.1 %ingest.1 = s32[32,2,640]{2,1,0:T(2,128)} custom-call(s32[64,128]{1,0:T(8,128)} %bitcast.52, s32[64,128]{1,0:T(8,128)} %bitcast.53, s32[7680,128]{1,0:T(8,128)} %bitcast.48), custom_call_target="tpu_custom_call" | custom-call | tf_op jit(solution)/shard_map/ingest/pallas_call | solution.py:103
  13.8 7.3 %all-to-all-start = ((s32[32,2,640]{2,1,0:T(2,128)}), s32[32,2,640]{2,1,0:T(2,128)S(1)}, u32[]{:S(2)}, u32[]{:S(2)}) async-start(s32[32,2,640]{2,1,0:T(2,128)} %ingest.1), calls=%async_computation | async-start | bytes 327680 | tf_op jit(solution)/shard_map/all_to_all | solution.py:259
  21.1 8.0 %all-to-all-done = s32[32,2,640]{2,1,0:T(2,128)S(1)} async-done(((s32[32,2,640]{2,1,0:T(2,128)}), s32[32,2,640]{2,1,0:T(2,128)S(1)}, u32[]{:S(2)}, u32[]{:S(2)}) %all-to-all-start) | async-done | bytes 163872 | tf_op jit(solution)/shard_map/all_to_all | solution.py:259
  29.1 0.9 %compare_select_fusion = s32[32,1,640]{2,1,0:T(1,128)} fusion(s32[32,2,640]{2,1,0:T(2,128)S(1)} %all-to-all-done), kind=kLoop, calls=%fused_computation | loop fusion | flops 245760 | bytes 245760 | tf_op jit(solution)/shard_map/jit(_where)/select_n | solution.py:262
  30.0 36.3 %scatter.1 = (f32[16384,128]{1,0:T(8,128)}, f32[32,8,128]{2,1,0:T(8,128)}, f32[128,8,128]{2,1,0:T(8,128)}) custom-call(s32[160,128]{1,0:T(8,128)} %bitcast.51, s32[2,128]{1,0:T(2,128)} %proposals.1, f32[16384,128]{1,0:T(8,128)} %bitcast.47), custom_call_target="tpu_custom_call" | custom-call | tf_op jit(solution)/shard_map/scatter/pallas_call | solution.py:218
  66.3 1.0 %dynamic-slice_bitcast_fusion = f32[2,32,8,128]{3,2,1,0:T(8,128)S(1)} fusion(f32[2,2,32,8,128]{4,3,2,1,0:T(8,128)} %bitcast.49, s32[]{:T(128)S(6)} %select_n.51), kind=kLoop, calls=%fused_computation.2 | loop fusion | bytes 524292 | tf_op jit(solution)/shard_map/jit(dynamic_index_in_dim)/squeeze | solution.py:274
  67.3 0.1 collective-permute-start
  67.5 1.4 %collective-permute-done = f32[2,32,8,128]{3,2,1,0:T(8,128)S(1)} collective-permute-done((f32[2,32,8,128]{3,2,1,0:T(8,128)S(1)}, f32[2,32,8,128]{3,2,1,0:T(8,128)S(1)}, u32[]{:S(2)}, u32[]{:S(2)}) %collective-permute-start) | collective-permute-done | bytes 262176 | tf_op jit(solution)/shard_map/ppermute | solution.py:273
  68.9 1.0 %bitcast_add_fusion = f32[2,32,8,128]{3,2,1,0:T(8,128)S(1)} fusion(f32[2,32,8,128]{3,2,1,0:T(8,128)S(1)} %collective-permute-done, f32[2,2,32,8,128]{4,3,2,1,0:T(8,128)} %bitcast.50, s32[]{:T(128)S(6)} %select_n.50), kind=kLoop, calls=%fused_computation.1 | loop fusion | flops 65536 | bytes 786436 | tf_op jit(solution)/shard_map/add | solution.py:278
  69.9 0.2 collective-permute-start.1
  70.1 0.1 broadcast_in_dim.52
  70.2 0.1 broadcast_in_dim.53
  70.3 5.2 %collective-permute-done.1 = f32[1,32,8,128]{3,2,1,0:T(8,128)S(1)} collective-permute-done((f32[1,32,8,128]{3,2,1,0:T(8,128)S(1)}, f32[1,32,8,128]{3,2,1,0:T(8,128)S(1)}, u32[]{:S(2)}, u32[]{:S(2)}) %collective-permute-start.1) | collective-permute-done | bytes 131104 | tf_op jit(solution)/shard_map/ppermute | solution.py:273
  75.5 0.3 fusion.9
  75.8 1.9 %fusion.5 = (f32[32]{0:T(128)S(1)}, f32[32]{0:T(128)S(1)}, f32[32]{0:T(128)S(1)}, f32[32]{0:T(128)S(1)}, f32[32]{0:T(128)S(1)}) fusion(f32[1,32,8,128]{3,2,1,0:T(8,128)S(1)} %get-tuple-element.17, s32[32]{0:T(128)S(1)} %get-tuple-element.19, s32[8]{0:T(128)S(1)} %multiply_add_fusion, f32[32,8,128]{2,1,0:T(8,128)} %get-tuple-element.7, ...), kind=kLoop, calls=%fused_computation.13 | loop fusion | flops 720736 | bytes 263072 | tf_op jit(solution)/shard_map/reduce_sum | solution.py:295
  77.7 0.1 stack.21
  77.8 0.1 stack.22
  77.9 0.1 stack.23
  78.0 0.1 stack.24
  78.0 0.1 stack.25
  78.1 0.1 stack.26
  78.2 0.1 reshape.111
  78.4 10.3 %all_to_all.10 = f32[32,1,128]{2,1,0:T(1,128)S(1)} all-to-all(f32[32,1,128]{2,1,0:T(1,128)S(1)} %bitcast.54), channel_id=1, replica_groups=mesh['row'=4,'col'=8] {'row','col'}, dimensions={0} | all-to-all | bytes 32768 | tf_op jit(solution)/shard_map/all_to_all | solution.py:309
  88.7 0.6 compare_select_fusion.1
  (21 shorter events, 0.3 us)
Async XLA Ops:
  0.6 66.8 %copy-start = (s32[2,128]{1,0:T(2,128)S(1)}, s32[2,128]{1,0:T(2,128)}, u32[]{:S(2)}) copy-start(s32[2,128]{1,0:T(2,128)} %proposals.1) | copy-start | bytes 3076
  0.6 88.1 %copy-start.1 = (s32[16]{0:T(128)S(1)}, s32[16]{0:T(128)}, u32[]{:S(2)}) copy-start(s32[16]{0:T(128)} %param.9) | copy-start | bytes 196
  13.8 15.3 %all-to-all-start = ((s32[32,2,640]{2,1,0:T(2,128)}), s32[32,2,640]{2,1,0:T(2,128)S(1)}, u32[]{:S(2)}, u32[]{:S(2)}) async-start(s32[32,2,640]{2,1,0:T(2,128)} %ingest.1), calls=%async_computation | async-start | bytes 327680 | tf_op jit(solution)/shard_map/all_to_all | solution.py:259
  67.3 1.6 %collective-permute-start = (f32[2,32,8,128]{3,2,1,0:T(8,128)S(1)}, f32[2,32,8,128]{3,2,1,0:T(8,128)S(1)}, u32[]{:S(2)}, u32[]{:S(2)}) collective-permute-start(f32[2,32,8,128]{3,2,1,0:T(8,128)S(1)} %dynamic-slice_bitcast_fusion), channel_id=1, source_target_pairs={{0,8},{8,0},{16,24},{24,16},{1,9},{9,1},{17,25},{25,17},{2,10},{10... | collective-permute-start | bytes 786440 | tf_op jit(solution)/shard_map/ppermute | solution.py:273
  69.9 5.6 %collective-permute-start.1 = (f32[1,32,8,128]{3,2,1,0:T(8,128)S(1)}, f32[1,32,8,128]{3,2,1,0:T(8,128)S(1)}, u32[]{:S(2)}, u32[]{:S(2)}) collective-permute-start(f32[1,32,8,128]{3,2,1,0:T(8,128)S(1)} %constant_dynamic-slice_fusion), channel_id=1, source_target_pairs={{0,16},{8,24},{16,0},{24,8},{1,17},{9,25},{17,1},{25,9},{2,18},{10... | collective-permute-start | bytes 393224 | tf_op jit(solution)/shard_map/ppermute | solution.py:273

commit v4 on v3

v4 whole, which is shorter than its diff:
```python
import functools

import jax
import jax.numpy as jnp
from jax import lax
from jax.experimental import pallas as pl
from jax.experimental.pallas import tpu as pltpu
from jax.sharding import PartitionSpec as P

COPIES = 5
GROUP = 8
SPARE = 32


def entropy_term(value):
    return value * jnp.log(jnp.maximum(value, 1.0))


def log2_of(size):
    assert size & (size - 1) == 0
    return size.bit_length() - 1


def ingest_kernel(
    rows_shift,
    cols_shift,
    col_shift,
    devices,
    ids_ref,
    table_hbm,
    out_ref,
    table_ref,
    lines_ref,
    lines_smem,
    picked,
    placed,
    sem_table,
    sem_lines,
):
    blocks = ids_ref.shape[0]
    slots = placed.shape[0]
    group = picked.shape[0] // 128
    rows_mask = (1 << rows_shift) - 1
    cols_mask = (1 << cols_shift) - 1

    def pick(index):
        for k in range(group):
            for lane in range(128):
                line = pl.ds(lines_smem[index * group + k, lane], 1)
                picked[k * 128 + lane : k * 128 + lane + 1, :] = table_ref[line, :]

    whole_table = pltpu.make_async_copy(table_hbm, table_ref, sem_table)
    whole_table.start()
    lines_ref[...] = ids_ref[...] >> 7
    lines = pltpu.make_async_copy(lines_ref, lines_smem, sem_lines)
    lines.start()
    placed[...] = jnp.zeros_like(placed)
    sublane = lax.broadcasted_iota(jnp.int32, (128, 128), 0)
    depth = lax.broadcasted_iota(jnp.int32, (128, 256), 0)
    width = lax.broadcasted_iota(jnp.int32, (128, 256), 1)
    upto = jnp.where((depth <= width) | (width >= 128), 1.0, 0.0).astype(jnp.bfloat16)
    owner_ids = lax.broadcasted_iota(jnp.int32, (devices, 128), 0)
    slot_ids = lax.broadcasted_iota(jnp.int32, (slots, 128), 0)
    steps = blocks // group
    lines.wait()
    whole_table.wait()
    pick(0)

    def place(index, carry, last=False):
        turned = [picked[k * 128 : (k + 1) * 128, :].T for k in range(group)]
        if not last:
            pick(index + 1)
        label = [
            jnp.sum(
                jnp.where(sublane == (ids_ref[pl.ds(index * group + k, 1), :] & 127), turned[k], 0),
                axis=0,
                keepdims=True,
            )
            for k in range(group)
        ]
        row = jnp.concatenate(label, axis=0)
        col = jnp.concatenate([label[k ^ 1] for k in range(group)], axis=0)
        owner = ((row >> rows_shift) << col_shift) + (col >> cols_shift)
        hot = [owner_ids == owner[k : k + 1, :] for k in range(group)]
        counted = jnp.dot(
            jnp.concatenate([jnp.where(h, 1.0, 0.0).astype(jnp.bfloat16) for h in hot], axis=0),
            upto,
            preferred_element_type=jnp.float32,
        )
        row_value = (row & rows_mask) + 1
        col_value = (col & cols_mask) + 1
        digits = [
            digit.astype(jnp.float32)
            for digit in (row_value >> 6, row_value & 63, col_value >> 6, col_value & 63)
        ]
        slot_parts = []
        digit_parts = []
        for k in range(group):
            part = counted[k * devices : (k + 1) * devices, :]
            rank = jnp.sum(jnp.where(hot[k], part[:, :128] + carry, 0.0), axis=0, keepdims=True)
            carry = carry + part[:, 128:]
            slot_parts.append(
                jnp.where(slot_ids == rank.astype(jnp.int32) - 1, 1.0, 0.0).astype(jnp.bfloat16)
            )
            digit_parts.append(
                jnp.concatenate(
                    [jnp.where(hot[k], d[k : k + 1, :], 0.0).astype(jnp.bfloat16) for d in digits],
                    axis=0,
                )
            )
        placed[...] += lax.dot_general(
            jnp.concatenate(slot_parts, axis=1),
            jnp.concatenate(digit_parts, axis=1),
            (((1,), (1,)), ((), ())),
            preferred_element_type=jnp.float32,
        )
        return carry

    place(steps - 1, lax.fori_loop(0, steps - 1, place, jnp.zeros((devices, 128), jnp.float32)), last=True)
    flat = placed[...].T.astype(jnp.int32)
    out_ref[:, 0, :] = flat[:devices] * 64 + flat[devices : 2 * devices] - 1
    out_ref[:, 1, :] = flat[2 * devices : 3 * devices] * 64 + flat[3 * devices :] - 1


def ingest(labels, edge_tiles, rows_tile, cols_tile, col_devices, devices, slots):
    ids = edge_tiles.reshape(-1, 128)
    table = labels.reshape(-1, 128)
    return pl.pallas_call(
        functools.partial(
            ingest_kernel, log2_of(rows_tile), log2_of(cols_tile), log2_of(col_devices), devices
        ),
        out_shape=jax.ShapeDtypeStruct((devices, 2, slots), jnp.int32),
        in_specs=[pl.BlockSpec(memory_space=pltpu.VMEM), pl.BlockSpec(memory_space=pl.ANY)],
        out_specs=pl.BlockSpec(memory_space=pltpu.VMEM),
        scratch_shapes=[
            pltpu.VMEM(table.shape, jnp.int32),
            pltpu.VMEM(ids.shape, jnp.int32),
            pltpu.SMEM(ids.shape, jnp.int32),
            pltpu.VMEM((GROUP * 128, 128), jnp.int32),
            pltpu.VMEM((slots, 4 * devices), jnp.float32),
            pltpu.SemaphoreType.DMA,
            pltpu.SemaphoreType.DMA,
        ],
        name="ingest",
    )(ids, table)


def scatter_kernel(
    capacity,
    arrived,
    proposals_hbm,
    counts,
    out,
    source_rows,
    kept_rows,
    sent_rows,
    copies,
    main,
    words_ref,
    words,
    proposals,
    source_ref,
    kept_ref,
    sent_ref,
    sem_counts,
    sem_words,
    sem_proposals,
    sem_rows,
    sem_out,
):
    total = counts.shape[0]
    senders = arrived.shape[0]
    parts = arrived.shape[2] // 128
    cols_tiles = source_ref.shape[1]
    arrive = pltpu.make_async_copy(counts, main.at[pl.ds(0, total)], sem_counts)
    arrive.start()
    asked = pltpu.make_async_copy(proposals_hbm, proposals, sem_proposals)
    asked.start()
    spare = total + (lax.broadcasted_iota(jnp.int32, (senders, 128), 1) & (SPARE - 1))
    spare = spare << 7
    for part in range(parts):
        row = arrived[:, 0, part * 128 : (part + 1) * 128]
        col = arrived[:, 1, part * 128 : (part + 1) * 128]
        line = (((row >> 3) * cols_tiles + (col >> 7)) << 3) + (row & 7)
        words_ref[pl.ds(part, senders, stride=parts), :] = jnp.where(
            row >= 0, (line << 7) + (col & 127), spare
        )
    listed = pltpu.make_async_copy(words_ref, words, sem_words)
    listed.start()
    zeros = jnp.zeros((256, 128), jnp.float32)
    for copy in copies:

        @pl.loop(0, total // 256)
        def _(i):
            copy[pl.ds(pl.multiple_of(i * 256, 256), 256), :] = zeros

    asked.wait()
    listed.wait()
    arrive.wait()
    lanes = lax.broadcasted_iota(jnp.int32, (1, 128), 1)
    sums = (main,) + tuple(copies)

    def add_line(at, count):
        for slot in range(count):
            word = words[at, slot]
            line = pl.ds(lax.shift_right_logical(word, 7), 1)
            hot = (jnp.full((1, 128), word, jnp.int32) & 127) == lanes
            sums[slot % len(sums)][line, :] += jnp.where(hot, 1.0, 0.0)

    whole, rest = capacity // 128, capacity % 128

    @pl.loop(0, senders)
    def _(sender):
        if whole:

            @pl.loop(0, whole)
            def _(part):
                add_line(sender * parts + part, 128)

        if rest:
            add_line(sender * parts + whole, rest)

    rows_tile = total // cols_tiles
    first = lax.axis_index("row") * rows_tile
    mine = source_ref.shape[0]
    offset = lax.axis_index("row") * mine

    def summed(row):
        at = pl.ds(((row >> 3) * cols_tiles << 3) + (row & 7), cols_tiles, stride=8)
        value = sums[0][at, :]
        for one in sums[1:]:
            value = value + one[at, :]
        return value

    @pl.loop(0, mine, unroll=8)
    def _(p):
        source_ref[p] = summed(proposals[0, offset + p] - first)

    side = lax.axis_index("row") & 1
    for rows, parity in ((kept_ref, side), (sent_ref, 1 - side)):

        @pl.loop(0, rows.shape[0], unroll=8)
        def _(q):
            block = lax.div(q, mine)
            row = proposals[1, (block + parity) * mine + q] - first
            here = (row >= 0) & (row < rows_tile)
            rows[q] = summed(jnp.where(here, row, 0)) * jnp.where(here, 1.0, 0.0)

    picked = [
        pltpu.make_async_copy(here, there, sem_rows.at[n])
        for n, (here, there) in enumerate(
            ((source_ref, source_rows), (kept_ref, kept_rows), (sent_ref, sent_rows))
        )
    ]
    for copy in picked:
        copy.start()
    chunk = total // 8
    for n in range(8):

        @pl.loop(0, chunk // 64)
        def _(i):
            at = pl.ds(pl.multiple_of(n * chunk + i * 64, 64), 64)
            value = main[at, :]
            for copy in copies:
                value = value + copy[at, :]
            main[at, :] = value

        at = pl.ds(n * chunk, chunk)
        pltpu.make_async_copy(main.at[at], out.at[at], sem_out).start()

    for copy in picked:
        copy.wait()
    pltpu.make_async_copy(main.at[pl.ds(0, total)], out, sem_out).wait()


def scatter(counts, arrived, proposals, capacity, row_devices):
    rows_tile, cols_tile = counts.shape
    cols_tiles = cols_tile // 128
    lines = counts.reshape(rows_tile // 8, 8, cols_tiles, 128).transpose(0, 2, 1, 3).reshape(-1, 128)
    total = lines.shape[0]
    count = proposals.shape[1]
    slots = (arrived.shape[0] * arrived.shape[2] // 128, 128)
    rows_shapes = [(size, cols_tiles, 128) for size in (count // row_devices, count // 2, count // 2)]
    out, source_rows, kept_rows, sent_rows = pl.pallas_call(
        functools.partial(scatter_kernel, capacity),
        out_shape=[jax.ShapeDtypeStruct(shape, jnp.float32) for shape in [lines.shape] + rows_shapes],
        in_specs=[
            pl.BlockSpec(memory_space=pltpu.VMEM),
            pl.BlockSpec(memory_space=pl.ANY),
            pl.BlockSpec(memory_space=pl.ANY),
        ],
        out_specs=[pl.BlockSpec(memory_space=pl.ANY)] * 4,
        scratch_shapes=[
            tuple(pltpu.VMEM((total + SPARE, 128), jnp.float32) for _ in range(COPIES - 1)),
            pltpu.VMEM((total + SPARE, 128), jnp.float32),
            pltpu.VMEM(slots, jnp.int32),
            pltpu.SMEM(slots, jnp.int32),
            pltpu.SMEM(proposals.shape, jnp.int32),
        ]
        + [pltpu.VMEM(shape, jnp.float32) for shape in rows_shapes]
        + [
            pltpu.SemaphoreType.DMA,
            pltpu.SemaphoreType.DMA,
            pltpu.SemaphoreType.DMA,
            pltpu.SemaphoreType.DMA((3,)),
            pltpu.SemaphoreType.DMA,
        ],
        compiler_params=pltpu.CompilerParams(vmem_limit_bytes=60000000),
        name="scatter",
    )(arrived, proposals, lines)
    updated = out.reshape(rows_tile // 8, cols_tiles, 8, 128).transpose(0, 2, 1, 3).reshape(rows_tile, cols_tile)
    return updated, source_rows, kept_rows, sent_rows


def terms_kernel(groups, cols_tile, proposals, own_ref, kept_ref, came_ref, out_ref):
    mine = own_ref.shape[0]
    per_col = mine // groups
    row_index = lax.axis_index("row")
    col_devices = lax.axis_size("col")
    shape = own_ref.shape[1:]
    position = (
        lax.axis_index("col") * cols_tile
        + 128 * lax.broadcasted_iota(jnp.int32, shape, 0)
        + lax.broadcasted_iota(jnp.int32, shape, 1)
    )
    zero = jnp.float32(0.0)
    lines = []
    for group in range(groups):
        columns = [[] for _ in range(6)]
        for k in range(per_col):
            p = group * per_col + k
            own = own_ref[p]
            other = kept_ref[p] + came_ref[p]
            at_source = position == proposals[0, row_index * mine + p]
            at_target = position == proposals[1, row_index * mine + p]
            mixed = entropy_term(own + other) - entropy_term(own) - entropy_term(other)
            values = (
                jnp.where(at_source | at_target, zero, mixed),
                jnp.where(at_source, own, zero),
                jnp.where(at_source, other, zero),
                jnp.where(at_target, other, zero),
                own,
                other,
            )
            for column, value in zip(columns, values):
                column.append(jnp.sum(value, axis=0, keepdims=True))
        rows = [row for column in columns for row in column]
        width = out_ref.shape[2]
        if len(rows) < width:
            rows.append(jnp.zeros((width - len(rows), 128), jnp.float32))
        lines.append(jnp.sum(jnp.concatenate(rows, axis=0).T, axis=0, keepdims=True))
    for device in range(out_ref.shape[0]):
        wanted, group = divmod(device % col_devices, groups)
        out_ref[device] = lines[group] * jnp.where(row_index == wanted, 1.0, 0.0)


def terms(proposals, own, kept, came, devices, cols_tile, per_col):
    width = -(-6 * per_col // 128) * 128
    return pl.pallas_call(
        functools.partial(terms_kernel, own.shape[0] // per_col, cols_tile),
        out_shape=jax.ShapeDtypeStruct((devices, 1, width), jnp.float32),
        in_specs=[pl.BlockSpec(memory_space=pltpu.SMEM)] + [pl.BlockSpec(memory_space=pltpu.VMEM)] * 3,
        out_specs=pl.BlockSpec(memory_space=pltpu.VMEM),
        name="terms",
    )(proposals, own, kept, came)


def per_device(counts, labels, edge_tiles, proposals, accept_flags):
    rows_tile, cols_tile = counts.shape
    row_devices = lax.axis_size("row")
    col_devices = lax.axis_size("col")
    devices = row_devices * col_devices
    edge_count = edge_tiles.shape[0] * edge_tiles.shape[2]
    capacity = 9 * edge_count // (2 * devices)
    slots = -(-capacity // 128) * 128
    outgoing = ingest(labels, edge_tiles, rows_tile, cols_tile, col_devices, devices, slots)
    arrived = lax.all_to_all(outgoing, ("row", "col"), split_axis=0, concat_axis=0, tiled=True)
    updated, own, kept, sent = scatter(counts, arrived, proposals, capacity, row_devices)

    mine = proposals.shape[1] // row_devices
    row_index = lax.axis_index("row")

    def swap(rows, bit):
        return lax.ppermute(rows, "row", [(device, device ^ (1 << bit)) for device in range(row_devices)])

    came = swap(sent, 0)
    for bit in range(1, log2_of(row_devices)):
        side = (row_index >> bit) & 1
        halves = (kept + came).reshape((-1, 2, mine) + kept.shape[1:])
        sent = lax.dynamic_index_in_dim(halves, 1 - side, 1, keepdims=False).reshape((-1,) + kept.shape[1:])
        kept = lax.dynamic_index_in_dim(halves, side, 1, keepdims=False).reshape((-1,) + kept.shape[1:])
        came = swap(sent, bit)
    per_col = accept_flags.shape[0]
    spread = terms(proposals, own, kept, came, devices, cols_tile, per_col)
    gathered = lax.all_to_all(spread, ("row", "col"), split_axis=0, concat_axis=0, tiled=True)
    sums = jnp.sum(gathered, axis=(0, 1))[: 6 * per_col].reshape(6, per_col)
    pair_sum, self_source, cross_count, self_target, degree_source, degree_target = sums
    corner = (
        entropy_term(self_source + 2.0 * cross_count + self_target)
        - entropy_term(self_source)
        - entropy_term(self_target)
        - 2.0 * entropy_term(cross_count)
    )
    change = (
        -(pair_sum + 0.5 * corner)
        + entropy_term(degree_source + degree_target)
        - entropy_term(degree_source)
        - entropy_term(degree_target)
    )
    merge_cost = change / (rows_tile * row_devices)
    accepted_cost = jnp.where(accept_flags == 1, merge_cost, jnp.float32(0.0))
    return (updated, merge_cost, accepted_cost)


def solution(mesh):
    return jax.shard_map(
        per_device,
        mesh=mesh,
        in_specs=(P("row", "col"), P(), P(("row", "col"), None, None), P(), P("col")),
        out_specs=(P("row", "col"), P("col"), P("col")),
        check_vma=False,
    )
```

time: 89.9 us -> 82.1 us (0.913)
  blocking collectives: 10.3 us -> 25.5 us
  waiting for transfers between devices: 14.7 us -> 5.96 us
  starting transfers between devices: 7.6 us -> 1.39 us
  Pallas kernels: 49.4 us -> 45.2 us
  other arithmetic: 4.82 us -> 1.64 us
    all_to_all x0 -> x1, blocking collectives: none -> 15.5 us  [per_device(): lax.all_to_all(outgoing, ('row', 'col'), split_axis=0, concat_axis=0, til...]
    all_to_all x1 -> x0, waiting for transfers between devices: 7.99 us -> none  [per_device(): lax.all_to_all(outgoing, ('row', 'col'), split_axis=0, concat_axis=0, til...]
    all_to_all x1 -> x0, starting transfers between devices: 7.32 us -> none  [per_device(): lax.all_to_all(outgoing, ('row', 'col'), split_axis=0, concat_axis=0, til...]
    pallas_call x1 -> x2, Pallas kernels: 36.3 us -> 33.8 us  [the longest x1 31.7 us: scatter(): pl.pallas_call(functools.partial(scatter_kernel, capacity), out_shape=[ja...]
    reduce_sum x3 -> x1, other arithmetic: 2.23 us -> 0.05 us  [per_device(): sums = jnp.sum(gathered, axis=(0, 1))[:6 * per_col].reshape(6, per_col)]
    pallas_call x1, Pallas kernels: 13.1 us -> 11.4 us  [ingest(): pl.pallas_call(functools.partial(ingest_kernel, log2_of(rows_tile), log2_...]
    ppermute x2, starting transfers between devices: 0.28 us -> 1.39 us  [swap(): lax.ppermute(rows, 'row', [(device, device ^ 1 << bit) for device in rang...]
    squeeze x2 -> x0, local copies, waits for them, and re-layouts: 1 us -> none  [per_device(): lax.dynamic_index_in_dim(halves, 1 - side, 1, keepdims=False)]
  transfers between devices with their start and end apart: 3 -> 2, of which waited for: 3 -> 2; matrix products, arithmetic and copies ran while one was open for 0% -> 0% of each run, Pallas kernels for 0% -> 0%
where the time goes in v4:
time: 82.1 us; the launch traced here: 81.7 us
  Pallas kernels  45.2 us (55%)
  blocking collectives  25.5 us (31%)
  waiting for transfers between devices  5.96 us (7%)
  other arithmetic  1.64 us (2%)
  starting transfers between devices  1.39 us (2%)
  local copies, waits for them, and re-layouts  1.33 us (2%)
    pallas_call x1, Pallas kernels, scatter(): pl.pallas_call(functools.partial(scatter_kernel, capacity), out_shape=[ja...  31.7 us
    all_to_all x1, blocking collectives, per_device(): lax.all_to_all(outgoing, ('row', 'col'), split_axis=0, concat_axis=0, til...  15.5 us
    pallas_call x1, Pallas kernels, ingest(): pl.pallas_call(functools.partial(ingest_kernel, log2_of(rows_tile), log2_...  11.4 us
    all_to_all x1, blocking collectives, per_device(): lax.all_to_all(spread, ('row', 'col'), split_axis=0, concat_axis=0, tiled...  10 us
    ppermute x2, waiting for transfers between devices, swap(): lax.ppermute(rows, 'row', [(device, device ^ 1 << bit) for device in rang...  5.96 us
    pallas_call x1, Pallas kernels, terms(): pl.pallas_call(functools.partial(terms_kernel, own.shape[0] // per_col, c...  2.04 us
  transfers between devices with their start and end apart: 2, of which 2 were waited for; matrix products, arithmetic and copies ran while one was open for 0% of the time, Pallas kernels for 0%

profile of v4, /device:TPU:0, one launch (start us, length us, event | category | flops | bytes accessed | tf_op | source)
XLA Modules:
  0.0 81.7 jit_solution(10352647229125877636)
XLA Ops:
  0.6 0.0 copy-start.1
  0.6 11.4 %ingest.1 = s32[32,2,640]{2,1,0:T(2,128)} custom-call(s32[64,128]{1,0:T(8,128)} %bitcast.20, s32[7680,128]{1,0:T(8,128)} %bitcast.18), custom_call_target="tpu_custom_call" | custom-call | tf_op jit(solution)/shard_map/ingest/pallas_call | solution.py:128
  12.1 15.5 %all_to_all.10.arrived = s32[32,2,640]{2,1,0:T(2,128)} all-to-all(s32[32,2,640]{2,1,0:T(2,128)} %ingest.1), channel_id=1, replica_groups=mesh['row'=4,'col'=8] {'row','col'}, dimensions={0} | all-to-all | bytes 327680 | tf_op jit(solution)/shard_map/all_to_all | solution.py:377
  27.5 31.7 %scatter.1 = (f32[16384,128]{1,0:T(8,128)}, f32[32,8,128]{2,1,0:T(8,128)}, f32[64,8,128]{2,1,0:T(8,128)}, f32[64,8,128]{2,1,0:T(8,128)}) custom-call(s32[32,2,640]{2,1,0:T(2,128)} %all_to_all.10.arrived, s32[2,128]{1,0:T(2,128)} %proposals.1, f32[16384,128]{1,0:T(8,128)} %bitcast.17), custom_call_target="tpu_custom_call" | custom-call | tf_op jit(solution)/shard_map/scatter/pallas_call | solution.py:284
  59.3 0.2 collective-permute-start
  59.5 1.6 %collective-permute-done = f32[64,8,128]{2,1,0:T(8,128)S(1)} collective-permute-done((f32[64,8,128]{2,1,0:T(8,128)}, f32[64,8,128]{2,1,0:T(8,128)S(1)}, u32[]{:S(2)}, u32[]{:S(2)}) %collective-permute-start) | collective-permute-done | bytes 262176 | tf_op jit(solution)/shard_map/ppermute | solution.py:384
  61.1 1.0 %add.26 = f32[64,8,128]{2,1,0:T(8,128)S(1)} add(f32[64,8,128]{2,1,0:T(8,128)} %get-tuple-element.9, f32[64,8,128]{2,1,0:T(8,128)S(1)} %collective-permute-done) | non-fusion elementwise | flops 65536 | bytes 786432 | tf_op jit(solution)/shard_map/add | solution.py:389
  62.1 0.7 dynamic-slice_bitcast_fusion
  62.8 1.2 %collective-permute-start.1 = (f32[32,8,128]{2,1,0:T(8,128)S(1)}, f32[32,8,128]{2,1,0:T(8,128)S(1)}, u32[]{:S(2)}, u32[]{:S(2)}) collective-permute-start(f32[32,8,128]{2,1,0:T(8,128)S(1)} %get-tuple-element.13), channel_id=1, source_target_pairs={{0,16},{8,24},{16,0},{24,8},{1,17},{9,25},{17,1},{25,9},{2,18},{10... | collective-permute-start | bytes 393224 | tf_op jit(solution)/shard_map/ppermute | solution.py:384
  63.9 4.3 %collective-permute-done.1.came_ref = f32[32,8,128]{2,1,0:T(8,128)S(1)} collective-permute-done((f32[32,8,128]{2,1,0:T(8,128)S(1)}, f32[32,8,128]{2,1,0:T(8,128)S(1)}, u32[]{:S(2)}, u32[]{:S(2)}) %collective-permute-start.1) | collective-permute-done | bytes 131104 | tf_op jit(solution)/shard_map/ppermute | solution.py:384
  68.3 0.0 copy-start
  68.3 0.6 copy-done
  68.9 2.0 %terms.1 = f32[32,1,128]{2,1,0:T(1,128)} custom-call(s32[2,128]{1,0:T(2,128)} %proposals.1, f32[32,8,128]{2,1,0:T(8,128)} %get-tuple-element.8.own_ref, f32[32,8,128]{2,1,0:T(8,128)} %get-tuple-element.14.kept_ref, f32[32,8,128]{2,1,0:T(8,128)} %copy-done), custom_call_target="tpu_custom_call" | custom-call | tf_op jit(solution)/shard_map/terms/pallas_call | solution.py:359
  71.0 10.0 %all_to_all.11 = f32[32,1,128]{2,1,0:T(1,128)S(1)} all-to-all(f32[32,1,128]{2,1,0:T(1,128)} %terms.1), channel_id=1, replica_groups=mesh['row'=4,'col'=8] {'row','col'}, dimensions={0} | all-to-all | bytes 32768 | tf_op jit(solution)/shard_map/all_to_all | solution.py:395
  81.0 0.1 reduce_sum.9
  81.0 0.0 copy-done.1
  81.0 0.6 compare_select_fusion
Async XLA Ops:
  0.6 80.4 %copy-start.1 = (s32[16]{0:T(128)S(1)}, s32[16]{0:T(128)}, u32[]{:S(2)}) copy-start(s32[16]{0:T(128)} %param.9) | copy-start | bytes 196
  59.3 1.8 %collective-permute-start = (f32[64,8,128]{2,1,0:T(8,128)}, f32[64,8,128]{2,1,0:T(8,128)S(1)}, u32[]{:S(2)}, u32[]{:S(2)}) collective-permute-start(f32[64,8,128]{2,1,0:T(8,128)} %get-tuple-element.10), channel_id=1, source_target_pairs={{0,8},{8,0},{16,24},{24,16},{1,9},{9,1},{17,25},{25,17},{2,10},{10... | collective-permute-start | bytes 786440 | tf_op jit(solution)/shard_map/ppermute | solution.py:384
  62.8 5.5 %collective-permute-start.1 = (f32[32,8,128]{2,1,0:T(8,128)S(1)}, f32[32,8,128]{2,1,0:T(8,128)S(1)}, u32[]{:S(2)}, u32[]{:S(2)}) collective-permute-start(f32[32,8,128]{2,1,0:T(8,128)S(1)} %get-tuple-element.13), channel_id=1, source_target_pairs={{0,16},{8,24},{16,0},{24,8},{1,17},{9,25},{17,1},{25,9},{2,18},{10... | collective-permute-start | bytes 393224 | tf_op jit(solution)/shard_map/ppermute | solution.py:384
  68.3 0.7 copy-start

commit v5 on v4

--- a/solution.py
+++ b/solution.py
@@ -7,7 +7,7 @@
 from jax.experimental.pallas import tpu as pltpu
 from jax.sharding import PartitionSpec as P
 
-COPIES = 5
+COPIES = 6
 GROUP = 8
 SPARE = 32
 
@@ -157,7 +157,9 @@
     copies,
     main,
     words_ref,
+    lanes_ref,
     words,
+    hot_ref,
     proposals,
     source_ref,
     kept_ref,
@@ -177,14 +179,13 @@
     asked = pltpu.make_async_copy(proposals_hbm, proposals, sem_proposals)
     asked.start()
     spare = total + (lax.broadcasted_iota(jnp.int32, (senders, 128), 1) & (SPARE - 1))
-    spare = spare << 7
     for part in range(parts):
         row = arrived[:, 0, part * 128 : (part + 1) * 128]
         col = arrived[:, 1, part * 128 : (part + 1) * 128]
         line = (((row >> 3) * cols_tiles + (col >> 7)) << 3) + (row & 7)
-        words_ref[pl.ds(part, senders, stride=parts), :] = jnp.where(
-            row >= 0, (line << 7) + (col & 127), spare
-        )
+        at = pl.ds(part, senders, stride=parts)
+        words_ref[at, :] = jnp.where(row >= 0, line, spare)
+        lanes_ref[at, :] = col & 127
     listed = pltpu.make_async_copy(words_ref, words, sem_words)
     listed.start()
     zeros = jnp.zeros((256, 128), jnp.float32)
@@ -197,28 +198,35 @@
     asked.wait()
     listed.wait()
     arrive.wait()
-    lanes = lax.broadcasted_iota(jnp.int32, (1, 128), 1)
     sums = (main,) + tuple(copies)
-
-    def add_line(at, count):
+    lane_ids = lax.broadcasted_iota(jnp.int32, (128, 128), 0)
+
+    def hot_lines(at):
+        return jnp.where(lane_ids == lanes_ref[pl.ds(at, 1), :], 1.0, 0.0).T
+
+    def add_line(at, then, count):
+        later = hot_lines(then)
         for slot in range(count):
-            word = words[at, slot]
-            line = pl.ds(lax.shift_right_logical(word, 7), 1)
-            hot = (jnp.full((1, 128), word, jnp.int32) & 127) == lanes
-            sums[slot % len(sums)][line, :] += jnp.where(hot, 1.0, 0.0)
+            line = pl.ds(words[at, slot], 1)
+            sums[slot % len(sums)][line, :] += hot_ref[slot : slot + 1, :]
+        hot_ref[...] = later
 
     whole, rest = capacity // 128, capacity % 128
+    hot_ref[...] = hot_lines(0)
 
     @pl.loop(0, senders)
     def _(sender):
+        following = jnp.minimum(sender + 1, senders - 1) * parts
         if whole:
 
             @pl.loop(0, whole)
             def _(part):
-                add_line(sender * parts + part, 128)
+                at = sender * parts + part
+                then = at + 1 if rest else jnp.where(part == whole - 1, following, at + 1)
+                add_line(at, then, 128)
 
         if rest:
-            add_line(sender * parts + whole, rest)
+            add_line(sender * parts + whole, following, rest)
 
     rows_tile = total // cols_tiles
     first = lax.axis_index("row") * rows_tile
@@ -294,7 +302,9 @@
             tuple(pltpu.VMEM((total + SPARE, 128), jnp.float32) for _ in range(COPIES - 1)),
             pltpu.VMEM((total + SPARE, 128), jnp.float32),
             pltpu.VMEM(slots, jnp.int32),
+            pltpu.VMEM(slots, jnp.int32),
             pltpu.SMEM(slots, jnp.int32),
+            pltpu.VMEM((128, 128), jnp.float32),
             pltpu.SMEM(proposals.shape, jnp.int32),
         ]
         + [pltpu.VMEM(shape, jnp.float32) for shape in rows_shapes]
@@ -386,9 +396,14 @@
     came = swap(sent, 0)
     for bit in range(1, log2_of(row_devices)):
         side = (row_index >> bit) & 1
-        halves = (kept + came).reshape((-1, 2, mine) + kept.shape[1:])
-        sent = lax.dynamic_index_in_dim(halves, 1 - side, 1, keepdims=False).reshape((-1,) + kept.shape[1:])
-        kept = lax.dynamic_index_in_dim(halves, side, 1, keepdims=False).reshape((-1,) + kept.shape[1:])
+
+        def half(rows, wanted):
+            rows = rows.reshape((-1, 2, mine) + rows.shape[1:])
+            rows = lax.dynamic_index_in_dim(rows, wanted, 1, keepdims=False)
+            return rows.reshape((-1,) + rows.shape[2:])
+
+        sent = half(kept, 1 - side) + half(came, 1 - side)
+        kept = half(kept, side) + half(came, side)
         came = swap(sent, bit)
     per_col = accept_flags.shape[0]
     spread = terms(proposals, own, kept, came, devices, cols_tile, per_col)

time: 82.1 us -> 79.3 us (0.966)
  Pallas kernels: 45.2 us -> 42.5 us
    pallas_call x1, Pallas kernels: 31.7 us -> 29 us  [scatter(): pl.pallas_call(functools.partial(scatter_kernel, capacity), out_shape=[ja...]
where the time goes in v5:
time: 79.3 us; the launch traced here: 78.9 us
  Pallas kernels  42.5 us (54%)
  blocking collectives  25.5 us (32%)
  waiting for transfers between devices  5.96 us (8%)
  other arithmetic  2.3 us (3%)
  starting transfers between devices  1.39 us (2%)
    pallas_call x1, Pallas kernels, scatter(): pl.pallas_call(functools.partial(scatter_kernel, capacity), out_shape=[ja...  29 us
    all_to_all x1, blocking collectives, per_device(): lax.all_to_all(outgoing, ('row', 'col'), split_axis=0, concat_axis=0, til...  15.4 us
    pallas_call x1, Pallas kernels, ingest(): pl.pallas_call(functools.partial(ingest_kernel, log2_of(rows_tile), log2_...  11.4 us
    all_to_all x1, blocking collectives, per_device(): lax.all_to_all(spread, ('row', 'col'), split_axis=0, concat_axis=0, tiled...  10 us
    ppermute x2, waiting for transfers between devices, swap(): lax.ppermute(rows, 'row', [(device, device ^ 1 << bit) for device in rang...  5.96 us
    pallas_call x1, Pallas kernels, terms(): pl.pallas_call(functools.partial(terms_kernel, own.shape[0] // per_col, c...  2.03 us
    add x1, other arithmetic, per_device(): sent = half(kept, 1 - side) + half(came, 1 - side)  1.64 us
  transfers between devices with their start and end apart: 2, of which 2 were waited for; matrix products, arithmetic and copies ran while one was open for 0% of the time, Pallas kernels for 0%

profile of v5, /device:TPU:0, one launch (start us, length us, event | category | flops | bytes accessed | tf_op | source)
XLA Modules:
  0.0 78.9 jit_solution(16425187579284459714)
XLA Ops:
  0.6 0.0 copy-start.1
  0.6 11.4 %ingest.1 = s32[32,2,640]{2,1,0:T(2,128)} custom-call(s32[64,128]{1,0:T(8,128)} %bitcast.22, s32[7680,128]{1,0:T(8,128)} %bitcast.19), custom_call_target="tpu_custom_call" | custom-call | tf_op jit(solution)/shard_map/ingest/pallas_call | solution.py:128
  12.1 15.4 %all_to_all.10.arrived = s32[32,2,640]{2,1,0:T(2,128)} all-to-all(s32[32,2,640]{2,1,0:T(2,128)} %ingest.1), channel_id=1, replica_groups=mesh['row'=4,'col'=8] {'row','col'}, dimensions={0} | all-to-all | bytes 327680 | tf_op jit(solution)/shard_map/all_to_all | solution.py:387
  27.5 29.0 %scatter.1 = (f32[16384,128]{1,0:T(8,128)}, f32[32,8,128]{2,1,0:T(8,128)}, f32[64,8,128]{2,1,0:T(8,128)}, f32[64,8,128]{2,1,0:T(8,128)}) custom-call(s32[32,2,640]{2,1,0:T(2,128)} %all_to_all.10.arrived, s32[2,128]{1,0:T(2,128)} %proposals.1, f32[16384,128]{1,0:T(8,128)} %bitcast.18), custom_call_target="tpu_custom_call" | custom-call | tf_op jit(solution)/shard_map/scatter/pallas_call | solution.py:292
  56.6 0.2 collective-permute-start
  56.8 1.6 %collective-permute-done = f32[64,8,128]{2,1,0:T(8,128)S(1)} collective-permute-done((f32[64,8,128]{2,1,0:T(8,128)}, f32[64,8,128]{2,1,0:T(8,128)S(1)}, u32[]{:S(2)}, u32[]{:S(2)}) %collective-permute-start) | collective-permute-done | bytes 262176 | tf_op jit(solution)/shard_map/ppermute | solution.py:394
  58.4 1.6 %add_bitcast_fusion = (f32[32,8,128]{2,1,0:T(8,128)S(1)}, f32[32,8,128]{2,1,0:T(8,128)}) fusion(f32[1,2,32,8,128]{4,3,2,1,0:T(8,128)S(1)} %bitcast.21, s32[]{:T(128)S(6)} %select_n.14, f32[1,2,32,8,128]{4,3,2,1,0:T(8,128)} %bitcast.20, s32[]{:T(128)S(6)} %select_n.13), kind=kLoop, calls=%fused_computation | loop fusion | flops 65536 | bytes 786440 | tf_op jit(solution)/shard_map/add | solution.py:405
  60.0 1.2 %collective-permute-start.1 = (f32[32,8,128]{2,1,0:T(8,128)S(1)}, f32[32,8,128]{2,1,0:T(8,128)S(1)}, u32[]{:S(2)}, u32[]{:S(2)}) collective-permute-start(f32[32,8,128]{2,1,0:T(8,128)S(1)} %get-tuple-element.13), channel_id=1, source_target_pairs={{0,16},{8,24},{16,0},{24,8},{1,17},{9,25},{17,1},{25,9},{2,18},{10... | collective-permute-start | bytes 393224 | tf_op jit(solution)/shard_map/ppermute | solution.py:394
  61.2 4.3 %collective-permute-done.1.came_ref = f32[32,8,128]{2,1,0:T(8,128)S(1)} collective-permute-done((f32[32,8,128]{2,1,0:T(8,128)S(1)}, f32[32,8,128]{2,1,0:T(8,128)S(1)}, u32[]{:S(2)}, u32[]{:S(2)}) %collective-permute-start.1) | collective-permute-done | bytes 131104 | tf_op jit(solution)/shard_map/ppermute | solution.py:394
  65.6 0.0 copy-start
  65.6 0.7 copy-done
  66.2 2.0 %terms.1 = f32[32,1,128]{2,1,0:T(1,128)} custom-call(s32[2,128]{1,0:T(2,128)} %proposals.1, f32[32,8,128]{2,1,0:T(8,128)} %get-tuple-element.8.own_ref, f32[32,8,128]{2,1,0:T(8,128)} %get-tuple-element.14.kept_ref, f32[32,8,128]{2,1,0:T(8,128)} %copy-done), custom_call_target="tpu_custom_call" | custom-call | tf_op jit(solution)/shard_map/terms/pallas_call | solution.py:369
  68.3 10.0 %all_to_all.11 = f32[32,1,128]{2,1,0:T(1,128)S(1)} all-to-all(f32[32,1,128]{2,1,0:T(1,128)} %terms.1), channel_id=1, replica_groups=mesh['row'=4,'col'=8] {'row','col'}, dimensions={0} | all-to-all | bytes 32768 | tf_op jit(solution)/shard_map/all_to_all | solution.py:410
  78.3 0.1 reduce_sum.9
  78.3 0.0 copy-done.1
  78.3 0.6 compare_select_fusion
Async XLA Ops:
  0.6 77.7 %copy-start.1 = (s32[16]{0:T(128)S(1)}, s32[16]{0:T(128)}, u32[]{:S(2)}) copy-start(s32[16]{0:T(128)} %param.9) | copy-start | bytes 196
  56.6 1.8 %collective-permute-start = (f32[64,8,128]{2,1,0:T(8,128)}, f32[64,8,128]{2,1,0:T(8,128)S(1)}, u32[]{:S(2)}, u32[]{:S(2)}) collective-permute-start(f32[64,8,128]{2,1,0:T(8,128)} %get-tuple-element.10), channel_id=1, source_target_pairs={{0,8},{8,0},{16,24},{24,16},{1,9},{9,1},{17,25},{25,17},{2,10},{10... | collective-permute-start | bytes 786440 | tf_op jit(solution)/shard_map/ppermute | solution.py:394
  60.0 5.5 %collective-permute-start.1 = (f32[32,8,128]{2,1,0:T(8,128)S(1)}, f32[32,8,128]{2,1,0:T(8,128)S(1)}, u32[]{:S(2)}, u32[]{:S(2)}) collective-permute-start(f32[32,8,128]{2,1,0:T(8,128)S(1)} %get-tuple-element.13), channel_id=1, source_target_pairs={{0,16},{8,24},{16,0},{24,8},{1,17},{9,25},{17,1},{25,9},{2,18},{10... | collective-permute-start | bytes 393224 | tf_op jit(solution)/shard_map/ppermute | solution.py:394
  65.6 0.7 copy-start

commit v6 on v5

--- a/solution.py
+++ b/solution.py
@@ -240,14 +240,14 @@
             value = value + one[at, :]
         return value
 
-    @pl.loop(0, mine, unroll=8)
+    @pl.loop(0, mine, unroll=16)
     def _(p):
         source_ref[p] = summed(proposals[0, offset + p] - first)
 
     side = lax.axis_index("row") & 1
     for rows, parity in ((kept_ref, side), (sent_ref, 1 - side)):
 
-        @pl.loop(0, rows.shape[0], unroll=8)
+        @pl.loop(0, rows.shape[0], unroll=16)
         def _(q):
             block = lax.div(q, mine)
             row = proposals[1, (block + parity) * mine + q] - first
@@ -322,7 +322,40 @@
     return updated, source_rows, kept_rows, sent_rows
 
 
-def terms_kernel(groups, cols_tile, proposals, own_ref, kept_ref, came_ref, out_ref):
+def terms_kernel(
+    groups,
+    cols_tile,
+    proposals_hbm,
+    own_hbm,
+    kept_hbm,
+    first_hbm,
+    last_hbm,
+    out_ref,
+    proposals,
+    own_ref,
+    kept_ref,
+    first_ref,
+    last_ref,
+    sems,
+):
+    top = log2_of(lax.axis_size("row")) - 1
+    half = pl.ds(((lax.axis_index("row") >> top) & 1) * own_ref.shape[0], own_ref.shape[0])
+    copies = [
+        pltpu.make_async_copy(there, here, sems.at[n])
+        for n, (there, here) in enumerate(
+            (
+                (proposals_hbm, proposals),
+                (own_hbm, own_ref),
+                (kept_hbm.at[half], kept_ref),
+                (first_hbm.at[half], first_ref),
+                (last_hbm, last_ref),
+            )
+        )
+    ]
+    for copy in copies:
+        copy.start()
+    for copy in copies:
+        copy.wait()
     mine = own_ref.shape[0]
     per_col = mine // groups
     row_index = lax.axis_index("row")
@@ -340,7 +373,7 @@
         for k in range(per_col):
             p = group * per_col + k
             own = own_ref[p]
-            other = kept_ref[p] + came_ref[p]
+            other = kept_ref[p] + first_ref[p] + last_ref[p]
             at_source = position == proposals[0, row_index * mine + p]
             at_target = position == proposals[1, row_index * mine + p]
             mixed = entropy_term(own + other) - entropy_term(own) - entropy_term(other)
@@ -364,15 +397,19 @@
         out_ref[device] = lines[group] * jnp.where(row_index == wanted, 1.0, 0.0)
 
 
-def terms(proposals, own, kept, came, devices, cols_tile, per_col):
+def terms(proposals, own, kept, first, last, devices, cols_tile, per_col):
     width = -(-6 * per_col // 128) * 128
     return pl.pallas_call(
         functools.partial(terms_kernel, own.shape[0] // per_col, cols_tile),
         out_shape=jax.ShapeDtypeStruct((devices, 1, width), jnp.float32),
-        in_specs=[pl.BlockSpec(memory_space=pltpu.SMEM)] + [pl.BlockSpec(memory_space=pltpu.VMEM)] * 3,
+        in_specs=[pl.BlockSpec(memory_space=pl.ANY)] * 5,
         out_specs=pl.BlockSpec(memory_space=pltpu.VMEM),
+        scratch_shapes=[pltpu.SMEM(proposals.shape, jnp.int32)]
+        + [pltpu.VMEM(own.shape, jnp.float32)] * 4
+        + [pltpu.SemaphoreType.DMA((5,))],
+        compiler_params=pltpu.CompilerParams(vmem_limit_bytes=8 << 20),
         name="terms",
-    )(proposals, own, kept, came)
+    )(proposals, own, kept, first, last)
 
 
 def per_device(counts, labels, edge_tiles, proposals, accept_flags):
@@ -393,20 +430,23 @@
     def swap(rows, bit):
         return lax.ppermute(rows, "row", [(device, device ^ (1 << bit)) for device in range(row_devices)])
 
+    def half(rows, wanted):
+        rows = rows.reshape((-1, 2, mine) + rows.shape[1:])
+        rows = lax.dynamic_index_in_dim(rows, wanted, 1, keepdims=False)
+        return rows.reshape((-1,) + rows.shape[2:])
+
+    bits = log2_of(row_devices)
+    assert bits > 1
     came = swap(sent, 0)
-    for bit in range(1, log2_of(row_devices)):
+    for bit in range(1, bits - 1):
         side = (row_index >> bit) & 1
-
-        def half(rows, wanted):
-            rows = rows.reshape((-1, 2, mine) + rows.shape[1:])
-            rows = lax.dynamic_index_in_dim(rows, wanted, 1, keepdims=False)
-            return rows.reshape((-1,) + rows.shape[2:])
-
         sent = half(kept, 1 - side) + half(came, 1 - side)
         kept = half(kept, side) + half(came, side)
         came = swap(sent, bit)
+    side = (row_index >> (bits - 1)) & 1
+    last = swap(half(kept, 1 - side) + half(came, 1 - side), bits - 1)
     per_col = accept_flags.shape[0]
-    spread = terms(proposals, own, kept, came, devices, cols_tile, per_col)
+    spread = terms(proposals, own, kept, came, last, devices, cols_tile, per_col)
     gathered = lax.all_to_all(spread, ("row", "col"), split_axis=0, concat_axis=0, tiled=True)
     sums = jnp.sum(gathered, axis=(0, 1))[: 6 * per_col].reshape(6, per_col)
     pair_sum, self_source, cross_count, self_target, degree_source, degree_target = sums

time: 79.3 us -> 78.6 us (level)
  local copies, waits for them, and re-layouts: 0.66 us -> 1.86 us
  Pallas kernels: 42.5 us -> 41.4 us
    unnamed x4 -> x8, local copies, waits for them, and re-layouts: 0.66 us -> 1.86 us
    pallas_call x1, Pallas kernels: 2.03 us -> 1.09 us  [terms(): pl.pallas_call(functools.partial(terms_kernel, own.shape[0] // per_col, c...]
where the time goes in v6:
time: 78.6 us; the launch traced here: 78.3 us
  Pallas kernels  41.4 us (53%)
  blocking collectives  25.3 us (32%)
  waiting for transfers between devices  5.95 us (8%)
  local copies, waits for them, and re-layouts  1.86 us (2%)
  other arithmetic  1.58 us (2%)
  starting transfers between devices  1.46 us (2%)
    pallas_call x1, Pallas kernels, scatter(): pl.pallas_call(functools.partial(scatter_kernel, capacity), out_shape=[ja...  28.9 us
    all_to_all x1, blocking collectives, per_device(): lax.all_to_all(outgoing, ('row', 'col'), split_axis=0, concat_axis=0, til...  15.5 us
    pallas_call x1, Pallas kernels, ingest(): pl.pallas_call(functools.partial(ingest_kernel, log2_of(rows_tile), log2_...  11.4 us
    all_to_all x1, blocking collectives, per_device(): lax.all_to_all(spread, ('row', 'col'), split_axis=0, concat_axis=0, tiled...  9.82 us
    ppermute x2, waiting for transfers between devices, swap(): lax.ppermute(rows, 'row', [(device, device ^ 1 << bit) for device in rang...  5.95 us
    unnamed x8, local copies, waits for them, and re-layouts  1.86 us
  transfers between devices with their start and end apart: 2, of which 2 were waited for; matrix products, arithmetic and copies ran while one was open for 0% of the time, Pallas kernels for 0%

profile of v6, /device:TPU:0, one launch (start us, length us, event | category | flops | bytes accessed | tf_op | source)
XLA Modules:
  0.0 78.3 jit_solution(7163742839140460152)
XLA Ops:
  0.6 0.0 copy-start.2
  0.6 0.0 copy-start.3
  0.7 11.4 %ingest.1 = s32[32,2,640]{2,1,0:T(2,128)} custom-call(s32[64,128]{1,0:T(8,128)} %bitcast.20, s32[7680,128]{1,0:T(8,128)} %bitcast.19), custom_call_target="tpu_custom_call" | custom-call | tf_op jit(solution)/shard_map/ingest/pallas_call | solution.py:128
  12.1 15.5 %all_to_all.10.arrived = s32[32,2,640]{2,1,0:T(2,128)} all-to-all(s32[32,2,640]{2,1,0:T(2,128)} %ingest.1), channel_id=1, replica_groups=mesh['row'=4,'col'=8] {'row','col'}, dimensions={0} | all-to-all | bytes 327680 | tf_op jit(solution)/shard_map/all_to_all | solution.py:424
  27.6 28.9 %scatter.1 = (f32[16384,128]{1,0:T(8,128)}, f32[32,8,128]{2,1,0:T(8,128)}, f32[64,8,128]{2,1,0:T(8,128)}, f32[64,8,128]{2,1,0:T(8,128)}) custom-call(s32[32,2,640]{2,1,0:T(2,128)} %all_to_all.10.arrived, s32[2,128]{1,0:T(2,128)} %proposals_hbm.3, f32[16384,128]{1,0:T(8,128)} %bitcast.18), custom_call_target="tpu_custom_call" | custom-call | tf_op jit(solution)/shard_map/scatter/pallas_call | solution.py:292
  56.5 0.2 collective-permute-start
  56.7 1.6 %collective-permute-done.first_hbm = f32[64,8,128]{2,1,0:T(8,128)S(1)} collective-permute-done((f32[64,8,128]{2,1,0:T(8,128)}, f32[64,8,128]{2,1,0:T(8,128)S(1)}, u32[]{:S(2)}, u32[]{:S(2)}) %collective-permute-start) | collective-permute-done | bytes 262176 | tf_op jit(solution)/shard_map/ppermute | solution.py:431
  58.3 0.9 %add_bitcast_fusion = f32[32,8,128]{2,1,0:T(8,128)S(1)} fusion(f32[1,2,32,8,128]{4,3,2,1,0:T(8,128)S(1)} %bitcast.17, s32[]{:T(128)S(6)} %select_n.9, f32[1,2,32,8,128]{4,3,2,1,0:T(8,128)} %bitcast.16), kind=kLoop, calls=%fused_computation | loop fusion | flops 32768 | bytes 393220 | tf_op jit(solution)/shard_map/add | solution.py:447
  59.2 1.3 %collective-permute-start.1 = (f32[32,8,128]{2,1,0:T(8,128)S(1)}, f32[32,8,128]{2,1,0:T(8,128)S(1)}, u32[]{:S(2)}, u32[]{:S(2)}) collective-permute-start(f32[32,8,128]{2,1,0:T(8,128)S(1)} %add_bitcast_fusion), channel_id=1, source_target_pairs={{0,16},{8,24},{16,0},{24,8},{1,17},{9,25},{17,1},{25,9},{2,18},{10... | collective-permute-start | bytes 393224 | tf_op jit(solution)/shard_map/ppermute | solution.py:431
  60.5 4.3 %collective-permute-done.1.last_hbm = f32[32,8,128]{2,1,0:T(8,128)S(1)} collective-permute-done((f32[32,8,128]{2,1,0:T(8,128)S(1)}, f32[32,8,128]{2,1,0:T(8,128)S(1)}, u32[]{:S(2)}, u32[]{:S(2)}) %collective-permute-start.1) | collective-permute-done | bytes 131104 | tf_op jit(solution)/shard_map/ppermute | solution.py:431
  64.8 0.0 copy-done.2
  64.8 0.0 copy-start
  64.8 0.9 %copy-done = f32[64,8,128]{2,1,0:T(8,128)S(1)} copy-done((f32[64,8,128]{2,1,0:T(8,128)S(1)}, f32[64,8,128]{2,1,0:T(8,128)}, u32[]{:S(2)}) %copy-start) | copy-done | bytes 262168
  65.8 0.0 copy-start.1
  65.8 0.9 %copy-done.1 = f32[32,8,128]{2,1,0:T(8,128)S(1)} copy-done((f32[32,8,128]{2,1,0:T(8,128)S(1)}, f32[32,8,128]{2,1,0:T(8,128)}, u32[]{:S(2)}) %copy-start.1) | copy-done | bytes 131096
  66.7 1.1 %terms.1 = f32[32,1,128]{2,1,0:T(1,128)S(1)} custom-call(s32[2,128]{1,0:T(2,128)S(1)} %copy-done.2, f32[32,8,128]{2,1,0:T(8,128)S(1)} %copy-done.1, f32[64,8,128]{2,1,0:T(8,128)S(1)} %copy-done, f32[64,8,128]{2,1,0:T(8,128)S(1)} %collective-permute-done.first_hbm, f32[32,8,128]{2,1,0:T(8,128)S(1)} %collective-permute-done.1.last_hbm), custom_call_target="tpu_custom_call" | custom-call | tf_op jit(solution)/shard_map/terms/pallas_call | solution.py:402
  67.8 9.8 %all_to_all.11 = f32[32,1,128]{2,1,0:T(1,128)S(1)} all-to-all(f32[32,1,128]{2,1,0:T(1,128)S(1)} %terms.1), channel_id=1, replica_groups=mesh['row'=4,'col'=8] {'row','col'}, dimensions={0} | all-to-all | bytes 32768 | tf_op jit(solution)/shard_map/all_to_all | solution.py:450
  77.6 0.1 reduce_sum.9
  77.6 0.0 copy-done.3
  77.6 0.6 compare_select_fusion
Async XLA Ops:
  0.6 64.2 %copy-start.2 = (s32[2,128]{1,0:T(2,128)S(1)}, s32[2,128]{1,0:T(2,128)}, u32[]{:S(2)}) copy-start(s32[2,128]{1,0:T(2,128)} %proposals_hbm.3) | copy-start | bytes 3076
  0.6 77.0 %copy-start.3 = (s32[16]{0:T(128)S(1)}, s32[16]{0:T(128)}, u32[]{:S(2)}) copy-start(s32[16]{0:T(128)} %param.9) | copy-start | bytes 196
  56.5 1.8 %collective-permute-start = (f32[64,8,128]{2,1,0:T(8,128)}, f32[64,8,128]{2,1,0:T(8,128)S(1)}, u32[]{:S(2)}, u32[]{:S(2)}) collective-permute-start(f32[64,8,128]{2,1,0:T(8,128)} %get-tuple-element.10), channel_id=1, source_target_pairs={{0,8},{8,0},{16,24},{24,16},{1,9},{9,1},{17,25},{25,17},{2,10},{10... | collective-permute-start | bytes 786440 | tf_op jit(solution)/shard_map/ppermute | solution.py:431
  59.2 5.6 %collective-permute-start.1 = (f32[32,8,128]{2,1,0:T(8,128)S(1)}, f32[32,8,128]{2,1,0:T(8,128)S(1)}, u32[]{:S(2)}, u32[]{:S(2)}) collective-permute-start(f32[32,8,128]{2,1,0:T(8,128)S(1)} %add_bitcast_fusion), channel_id=1, source_target_pairs={{0,16},{8,24},{16,0},{24,8},{1,17},{9,25},{17,1},{25,9},{2,18},{10... | collective-permute-start | bytes 393224 | tf_op jit(solution)/shard_map/ppermute | solution.py:431
  64.8 1.0 %copy-start = (f32[64,8,128]{2,1,0:T(8,128)S(1)}, f32[64,8,128]{2,1,0:T(8,128)}, u32[]{:S(2)}) copy-start(f32[64,8,128]{2,1,0:T(8,128)} %get-tuple-element.9.kept_hbm) | copy-start | bytes 786436
  65.8 0.9 %copy-start.1 = (f32[32,8,128]{2,1,0:T(8,128)S(1)}, f32[32,8,128]{2,1,0:T(8,128)}, u32[]{:S(2)}) copy-start(f32[32,8,128]{2,1,0:T(8,128)} %get-tuple-element.8.own_hbm) | copy-start | bytes 393220
